TPU v7x, 512 devices: a whole 4x4x16 slice. The times are simulated.
512 devices in a mesh: ctx: 64 (over y, z_hi, x), tp: 8 (over z_lo, core).
Axes of the slice: x: 4, y: 4, z: 16 (z_hi: 4, z_lo: 4; z = z_hi * 4 + z_lo), core: 2. Of those that a mesh axis runs over, the one named last changes fastest.
Arguments:
- queries: bfloat16 [8192, 4096], P('ctx', 'tp'), may hold values from -220 to 220
- keys: bfloat16 [8192, 1024], P('ctx', 'tp'), may hold values from -6 to 6
- values: bfloat16 [8192, 1024], P('ctx', 'tp'), may hold values from -6 to 6
- out_weight: bfloat16 [4096, 4096], P('tp'), may hold values from -0.09375 to 0.09375
- residual: bfloat16 [8192, 4096], P('ctx', 'tp'), may hold values from -1.5 to 1.5
- norm_gain: bfloat16 [4096], P('tp'), may hold values from 0.5 to 1.5
- span_order: int32 [128], replicated, may hold values from 0 to 127, as said below
Outputs:
- normed: bfloat16 [8192, 4096], P('ctx', 'tp')
Inputs may be any that keep to these rules, and one draw needn't show every extreme that they name: `span_order`: every span appears in exactly one slot. The two slots of one index d of ctx (slots 2d and 2d + 1) hold a span p and its mirror, the span at the same place counted from the end of the sequence; which index holds which pair, and the order of the two, are drawn.
All inputs are finite; a program needn't handle non-finite values.
Results may differ from a plain program's by a relative error of at most 0.009.
Values may be sent and summed in bfloat16 or wider, within the bound.
No kernel may reach another device: no remote copies, remote signals or barrier semaphores. Data moves between devices by JAX's collectives and lax.ppermute only.
A program may use at most 64 MiB of HBM per device.

v0:
```python
import math

import jax
import jax.numpy as jnp
from jax import lax
from jax.sharding import PartitionSpec as P

D = 4096
HEAD_SIZE = 128


EPSILON = 1e-05


def side_by_side(arrays, axis, dim, along):
    ends, at = ([], 0)
    for a in arrays[:-1]:
        at += a.shape[along]
        ends.append(at)
    both = jnp.concatenate(arrays, axis=along)
    return tuple(jnp.split(lax.all_gather(both, axis, axis=dim, tiled=True), ends, axis=along))


def cut_along(shard, dim, peers):
    lengths = shard.shape
    parts = shard.reshape(*lengths[:dim], peers, lengths[dim] // peers, *lengths[dim + 1 :])
    return jnp.moveaxis(parts, dim, 0)


def sent_and_summed(shard, axis, dim):
    peers = lax.axis_size(axis)
    parts = lax.all_to_all(cut_along(shard, dim, peers), axis, 0, 0, tiled=True)
    return jnp.sum(parts.astype(jnp.float32), axis=0)


def from_everyone(shard, axis):
    copies = jnp.broadcast_to(shard, (lax.axis_size(axis), *shard.shape))
    return lax.all_to_all(copies, axis, split_axis=0, concat_axis=0, tiled=True)


def of_everyone(shard, axis):
    return from_everyone(shard, axis).sum(axis=0)


def per_device(queries, keys, values, out_weight, residual, norm_gain, span_order):
    local_rows = queries.shape[0]
    span_rows = local_rows // 2
    heads = queries.shape[1] // HEAD_SIZE
    kv_heads = keys.shape[1] // HEAD_SIZE
    group_size = heads // kv_heads
    scale = 1.0 / math.sqrt(HEAD_SIZE)
    device = lax.axis_index("ctx")
    owned = lax.dynamic_slice_in_dim(span_order, 2 * device, 2)
    offsets = jnp.arange(span_rows, dtype=jnp.int32)
    query_pos = (owned[:, None] * span_rows + offsets[None, :]).reshape(local_rows)
    query_mat = queries.reshape(local_rows, kv_heads, group_size, HEAD_SIZE)
    fresh = (
        jnp.full((kv_heads, group_size, local_rows), -1e30, jnp.float32),
        jnp.zeros((kv_heads, group_size, local_rows), jnp.float32),
        jnp.zeros((kv_heads, group_size, local_rows, HEAD_SIZE), jnp.float32),
    )
    carry = fresh
    key_piece, value_piece = side_by_side((keys, values), "ctx", 0, 1)
    count = key_piece.shape[0]
    spans = count // span_rows
    per_step = max(1, min(spans, 1024 // span_rows))
    while spans % per_step != 0:
        per_step = per_step - 1
    steps = spans // per_step
    block_rows = per_step * span_rows
    key_pos_all = (span_order[:, None] * span_rows + offsets[None, :]).reshape(steps, block_rows)
    key_blocks = key_piece.reshape(steps, block_rows, kv_heads, HEAD_SIZE)
    value_blocks = value_piece.reshape(steps, block_rows, kv_heads, HEAD_SIZE)

    def scan_step(state, item):
        running, total, accum = state
        key_pos, key_mat, value_mat = item
        scores = (
            jnp.einsum("qhgd,khd->hgqk", query_mat, key_mat, preferred_element_type=jnp.float32)
            * scale
        )
        allowed = (key_pos[None, :] <= query_pos[:, None])[None, None, :, :]
        scores = jnp.where(allowed, scores, -1e30)
        newmax = jnp.maximum(running, jnp.max(scores, axis=-1))
        weights = jnp.where(allowed, jnp.exp(scores - newmax[..., None]), 0.0)
        fade = jnp.exp(running - newmax)
        total = total * fade + jnp.sum(weights, axis=-1)
        accum = accum * fade[..., None] + jnp.einsum(
            "hgqk,khd->hgqd",
            weights.astype(jnp.bfloat16),
            value_mat,
            preferred_element_type=jnp.float32,
        )
        return ((newmax, total, accum), None)

    carry, unused = lax.scan(scan_step, carry, (key_pos_all, key_blocks, value_blocks))
    running, total, accum = carry
    attended = accum / total[..., None]
    attended = (
        jnp.transpose(attended, (2, 0, 1, 3))
        .reshape(local_rows, heads * HEAD_SIZE)
        .astype(jnp.bfloat16)
    )
    partial_value = jnp.dot(attended, out_weight, preferred_element_type=jnp.float32)
    share = sent_and_summed(partial_value.astype(jnp.bfloat16), "tp", 1)
    hidden = (residual.astype(jnp.float32) + share).astype(jnp.bfloat16)
    hidden_f = hidden.astype(jnp.float32)
    squares = of_everyone(jnp.sum(hidden_f * hidden_f, axis=1), "tp")
    factor = lax.rsqrt(squares / D + EPSILON)
    normed = hidden_f * factor[:, None] * norm_gain.astype(jnp.float32)[None, :]
    return normed.astype(jnp.bfloat16)


def solution(mesh):
    return jax.shard_map(
        per_device,
        mesh=mesh,
        in_specs=(
            P("ctx", "tp"),
            P("ctx", "tp"),
            P("ctx", "tp"),
            P("tp", None),
            P("ctx", "tp"),
            P("tp"),
            P(),
        ),
        out_specs=P("ctx", "tp"),
        check_vma=False,
    )
```

profile of v0, /device:TPU:1, one launch (start us, length us, event | category | flops | bytes accessed | tf_op | source)
XLA Modules:
  0.0 245.0 jit_solution(17046809099755604104)
XLA Ops:
  6.5 1.4 pad_maximum_fusion
  8.0 1.0 copy.24
  9.0 0.1 copy.25
  9.2 0.7 broadcast_multiply_fusion
  10.2 0.7 dynamic-slice_multiply_fusion
  10.9 145.7 %all-gather.2.cloned.1.call-done = bf16[8192,256]{1,0:T(8,128)(2,1)} async-done(((bf16[128,256]{1,0:T(8,128)(2,1)}), bf16[8192,256]{1,0:T(8,128)(2,1)}) %all-gather.2.cloned.1.call-update) | async-done | bytes 4194320 | tf_op jit(solution)/shard_map/all_gather | solution.py:21
  156.6 4.5 %fusion.28 = (bf16[8192,128]{1,0:T(8,128)(2,1)}, bf16[8192,128]{1,0:T(8,128)(2,1)}) fusion(bf16[8192,256]{1,0:T(8,128)(2,1)} %all-gather.2.cloned.1.call-done), kind=kLoop, calls=%fused_computation.49 | loop fusion | bytes 8388608 | tf_op jit(solution)/shard_map/split | solution.py:21
  161.1 33.2 %while.15 = (s32[]{:T(128)}, f32[1,4,128]{2,1,0:T(4,128)S(1)}, f32[1,4,128]{2,1,0:T(4,128)S(1)}, f32[1,4,128,128]{3,2,1,0:T(8,128)S(1)}, s32[8,1024]{1,0:T(8,128...) while((s32[]{:T(128)}, f32[1,4,128]{2,1,0:T(4,128)S(1)}, ...), condition=%wide.region_3.4_spmd.clone, body=%wide.region_0.3_spmd.clone.sunk | while | flops 275582080 | bytes 8043653 | solution.py:96
  161.2 0.2 broadcast_compare_fusion.2
  161.5 1.4 fusion.39
  162.9 1.8 fusion.42
  164.6 0.5 fusion.41
  165.4 0.2 broadcast_compare_fusion.2
  165.6 1.4 fusion.39
  167.0 1.8 fusion.42
  168.8 0.5 fusion.41
  169.5 0.2 broadcast_compare_fusion.2
  169.8 1.4 fusion.39
  171.2 1.8 fusion.42
  172.9 0.5 fusion.41
  173.7 0.2 broadcast_compare_fusion.2
  173.9 1.4 fusion.39
  175.3 1.8 fusion.42
  177.1 0.5 fusion.41
  177.8 0.2 broadcast_compare_fusion.2
  178.1 1.4 fusion.39
  179.5 1.8 fusion.42
  181.2 0.5 fusion.41
  182.0 0.2 broadcast_compare_fusion.2
  182.2 1.4 fusion.39
  183.6 1.8 fusion.42
  185.4 0.5 fusion.41
  186.1 0.2 broadcast_compare_fusion.2
  186.4 1.4 fusion.39
  187.8 1.8 fusion.42
  189.5 0.5 fusion.41
  190.3 0.2 broadcast_compare_fusion.2
  190.5 1.4 fusion.39
  191.9 1.8 fusion.42
  193.7 0.5 fusion.41
  194.3 0.1 copy.26
  194.4 2.9 %convolution_convert_fusion = bf16[128,4096]{1,0:T(8,128)(2,1)S(1)} fusion(bf16[128,512]{0,1:T(8,128)(2,1)S(1)} %bitcast.96, bf16[512,4096]{1,0:T(8,128)(2,1)} %param.12), kind=kOutput, calls=%fused_computation.34 | convolution fusion | flops 537395200 | bytes 5373952 | tf_op jit(solution)/shard_map/dot_general | solution.py:104
  197.5 29.9 %all_to_all.11 = bf16[8,128,512]{2,1,0:T(8,128)(2,1)S(1)} all-to-all(bf16[8,128,512]{2,1,0:T(8,128)(2,1)S(1)} %bitcast.90), channel_id=1, replica_groups=mesh['ctx'=64,'tp'=8] {'tp'}, dimensions={0} | all-to-all | bytes 2097152 | tf_op jit(solution)/shard_map/all_to_all | solution.py:32
  227.4 0.1 convert_reduce_fusion
  227.7 0.6 broadcast_in_dim.44
  228.3 4.3 %all-to-all-start.1 = ((f32[8,1,128]{2,1,0:T(1,128)}), f32[8,1,128]{2,1,0:T(1,128)S(1)}, u32[]{:S(2)}, u32[]{:S(2)}) async-start(f32[8,1,128]{2,1,0:T(1,128)} %broadcast_in_dim.44), calls=%async_computation.1 | async-start | bytes 8192 | tf_op jit(solution)/shard_map/all_to_all | solution.py:38
  232.6 4.8 %all-to-all-done.1 = f32[8,1,128]{2,1,0:T(1,128)S(1)} async-done(((f32[8,1,128]{2,1,0:T(1,128)}), f32[8,1,128]{2,1,0:T(1,128)S(1)}, u32[]{:S(2)}, u32[]{:S(2)}) %all-to-all-start.1) | async-done | bytes 4128 | tf_op jit(solution)/shard_map/all_to_all | solution.py:38
  237.4 0.8 fusion.27
  (69 shorter events, 2.2 us)
Async XLA Ops:
  6.5 150.1 %all-gather.2.cloned.1.call-start = ((), (), s32[]{:S(2)}) async-start(), calls=%async_computation.2 | async-start | bytes 4259840 | tf_op jit(solution)/shard_map/all_gather | solution.py:21
  197.5 30.1 %copy-start = (bf16[128,512]{1,0:T(8,128)(2,1)S(1)}, bf16[128,512]{1,0:T(8,128)(2,1)}, u32[]{:S(2)}) copy-start(bf16[128,512]{1,0:T(8,128)(2,1)} %param.13) | copy-start | bytes 393220
  197.5 35.1 %copy-start.1 = (bf16[512]{0:T(512)(128)(2,1)S(1)}, bf16[512]{0:T(512)(128)(2,1)}, u32[]{:S(2)}) copy-start(bf16[512]{0:T(512)(128)(2,1)} %param.14) | copy-start | bytes 3076
  228.3 9.1 %all-to-all-start.1 = ((f32[8,1,128]{2,1,0:T(1,128)}), f32[8,1,128]{2,1,0:T(1,128)S(1)}, u32[]{:S(2)}, u32[]{:S(2)}) async-start(f32[8,1,128]{2,1,0:T(1,128)} %broadcast_in_dim.44), calls=%async_computation.1 | async-start | bytes 8192 | tf_op jit(solution)/shard_map/all_to_all | solution.py:38
Sparse Core Ops, SparseCore 0:
  11.5 145.0 all-gather.1
where the time goes:
time: 246 us; the launch traced here: 245 us
  waiting for transfers between devices  151 us (61%)
  blocking collectives  29.9 us (12%)
  matrix products  28.2 us (11%)
  between operations  13.5 us (5%)
  other arithmetic  10.6 us (4%)
  local copies, waits for them, and re-layouts  7.53 us (3%)
  starting transfers between devices  4.25 us (2%)
    all_gather x1, waiting for transfers between devices, side_by_side(): lax.all_gather(both, axis, axis=dim, tiled=True)  146 us
    all_to_all x1, blocking collectives, sent_and_summed(): parts = lax.all_to_all(cut_along(shard, dim, peers), axis, 0, 0, tiled=True)  29.9 us
    dot_general x8, matrix products, scan_step(): jnp.einsum('hgqk,khd->hgqd', weights.astype(jnp.bfloat16), value_mat, pre...  14.1 us
    dot_general x8, matrix products, scan_step(): jnp.einsum('qhgd,khd->hgqk', query_mat, key_mat, preferred_element_type=j...  11.2 us
  transfers between devices with their start and end apart: 2, of which 2 were waited for; matrix products, arithmetic and copies ran while one was open for 1% of the time, Pallas kernels for 0%

commit v1 on v0

v1 whole, which is shorter than its diff:
```python
import functools
import math

import jax
import jax.numpy as jnp
from jax import lax
from jax.experimental import pallas as pl
from jax.experimental.pallas import tpu as pltpu
from jax.sharding import Mesh, PartitionSpec as P

D = 4096
HEAD_SIZE = 128
EPSILON = 1e-05
SPAN = 64
HEADS = 4
NEG = -1e30
SCALE = 1.0 / math.sqrt(HEAD_SIZE)
LOG2E = math.log2(math.e)
STAT_ROWS = 16


def copies(shard, axis):
    stacked = jnp.broadcast_to(shard, (lax.axis_size(axis), *shard.shape))
    return lax.all_to_all(stacked, axis, split_axis=0, concat_axis=0, tiled=True)


def attention_kernel(qspan_ref, kspan_ref, q_ref, kv_ref, o_ref, vt_ref, s_ref):
    n_keys = kv_ref.shape[0]
    rows = HEADS * SPAN
    block = 256
    vt_ref[...] = kv_ref[:, HEAD_SIZE:].T
    diff = lax.broadcasted_iota(jnp.int32, (SPAN, rows), 0) - (
        lax.broadcasted_iota(jnp.int32, (SPAN, rows), 1) % SPAN
    )

    def tile(t, carry):
        peer = t // 2
        half = t % 2
        row0 = pl.multiple_of(half * SPAN, SPAN)
        qspan = qspan_ref[t]
        q = jnp.concatenate(
            [q_ref[peer, pl.ds(row0, SPAN), h * HEAD_SIZE : (h + 1) * HEAD_SIZE] for h in range(HEADS)],
            axis=0,
        )
        top = jnp.full((1, rows), NEG, jnp.float32)
        for b in range(n_keys // block):
            k = kv_ref[b * block : (b + 1) * block, :HEAD_SIZE]
            s = lax.dot_general(k, q, (((1,), (1,)), ((), ())), preferred_element_type=jnp.float32)
            for j in range(block // SPAN):
                n = b * (block // SPAN) + j
                limit = (qspan - kspan_ref[n]) * SPAN
                piece = jnp.where(diff <= limit, s[j * SPAN : (j + 1) * SPAN], NEG)
                s_ref[n * SPAN : (n + 1) * SPAN, :] = piece
                top = jnp.maximum(top, jnp.max(piece, axis=0, keepdims=True))
        total = jnp.zeros((1, rows), jnp.float32)
        acc = jnp.zeros((HEAD_SIZE, rows), jnp.float32)
        for b in range(n_keys // block):
            w = jnp.exp2((s_ref[b * block : (b + 1) * block, :] - top) * (SCALE * LOG2E))
            total = total + jnp.sum(w, axis=0, keepdims=True)
            acc = acc + jnp.dot(
                vt_ref[:, b * block : (b + 1) * block],
                w.astype(jnp.bfloat16),
                preferred_element_type=jnp.float32,
            )
        out = (acc / total).T.astype(jnp.bfloat16)
        for h in range(HEADS):
            o_ref[peer, pl.ds(row0, SPAN), h * HEAD_SIZE : (h + 1) * HEAD_SIZE] = out[h * SPAN : (h + 1) * SPAN]
        lse = top * SCALE + jnp.log(total)
        hi = lse.astype(jnp.bfloat16).astype(jnp.float32)
        mid = (lse - hi).astype(jnp.bfloat16).astype(jnp.float32)
        low = lse - hi - mid
        stats = jnp.concatenate([hi, mid, low, jnp.zeros((STAT_ROWS - 3, rows), jnp.float32)], axis=0)
        col0 = pl.multiple_of(half * rows, rows)
        o_ref[peer, 2 * SPAN :, pl.ds(col0, rows)] = stats.astype(jnp.bfloat16)
        return carry

    lax.fori_loop(0, 2 * q_ref.shape[0], tile, 0)


def attend(qspans, kspans, queries, kv):
    peers, local, width = queries.shape
    n_keys = kv.shape[0]
    vmem = pl.BlockSpec(memory_space=pltpu.VMEM)
    smem = pl.BlockSpec(memory_space=pltpu.SMEM)
    return pl.pallas_call(
        attention_kernel,
        out_shape=jax.ShapeDtypeStruct((peers, local + STAT_ROWS, width), jnp.bfloat16),
        in_specs=[smem, smem, vmem, vmem],
        out_specs=vmem,
        scratch_shapes=[
            pltpu.VMEM((HEAD_SIZE, n_keys), jnp.bfloat16),
            pltpu.VMEM((n_keys, HEADS * SPAN), jnp.float32),
        ],
        name="attend",
    )(qspans, kspans, queries, kv)


def combine_kernel(p_ref, o_ref):
    peers = p_ref.shape[0]
    width = p_ref.shape[2]
    lses = []
    for x in range(peers):
        st = p_ref[x, 2 * SPAN :, :].astype(jnp.float32)
        lses.append(st[0:1] + st[1:2] + st[2:3])
    top = functools.reduce(jnp.maximum, lses)
    ws = [jnp.exp(v - top) for v in lses]
    total = functools.reduce(jnp.add, ws)
    cols = jnp.concatenate([w / total for w in ws] + [jnp.zeros((8 - peers, width), jnp.float32)], axis=0).T
    for half in range(2):
        for h in range(HEADS):
            at = (half * HEADS + h) * SPAN
            out = jnp.zeros((SPAN, HEAD_SIZE), jnp.float32)
            for x in range(peers):
                part = p_ref[x, half * SPAN : (half + 1) * SPAN, h * HEAD_SIZE : (h + 1) * HEAD_SIZE]
                out = out + cols[at : at + SPAN, x : x + 1] * part.astype(jnp.float32)
            o_ref[half * SPAN : (half + 1) * SPAN, h * HEAD_SIZE : (h + 1) * HEAD_SIZE] = out.astype(jnp.bfloat16)


def combine(parts):
    peers, local, width = parts.shape
    vmem = pl.BlockSpec(memory_space=pltpu.VMEM)
    return pl.pallas_call(
        combine_kernel,
        out_shape=jax.ShapeDtypeStruct((2 * SPAN, width), jnp.bfloat16),
        in_specs=[vmem],
        out_specs=vmem,
        name="combine",
    )(parts)


def project_kernel(core_ref, own_ref, other_ref, w_ref, w2_ref, o_ref):
    out = jnp.dot(own_ref[...], w_ref[...], preferred_element_type=jnp.float32)
    out = out + jnp.dot(other_ref[...], w2_ref[...], preferred_element_type=jnp.float32)
    o_ref[0] = out.astype(jnp.bfloat16)


def project(core, own, other, weight, weight_other):
    rows, width = own.shape
    block = 512
    chips = weight.shape[1] // block // 2
    return pl.pallas_call(
        project_kernel,
        grid_spec=pltpu.PrefetchScalarGridSpec(
            num_scalar_prefetch=1,
            grid=(chips,),
            in_specs=[
                pl.BlockSpec((rows, width), lambda z, c: (0, 0)),
                pl.BlockSpec((rows, width), lambda z, c: (0, 0)),
                pl.BlockSpec((width, block), lambda z, c: (0, 2 * z + c[0])),
                pl.BlockSpec((width, block), lambda z, c: (0, 2 * z + c[0])),
            ],
            out_specs=pl.BlockSpec((1, rows, block), lambda z, c: (z, 0, 0)),
        ),
        out_shape=jax.ShapeDtypeStruct((chips, rows, block), jnp.bfloat16),
        name="project",
    )(core, own, other, weight, weight_other)


def per_device(queries, keys, values, out_weight, residual, norm_gain, span_order):
    y = lax.axis_index("y")
    zh = lax.axis_index("zh")
    x = lax.axis_index("x")
    core = lax.axis_index("c")
    spans = span_order.reshape(4, 4, 4, 2)
    qspans = lax.dynamic_slice(spans, (y, zh, 0, 0), (1, 1, 4, 2)).reshape(8)
    kspans = lax.dynamic_slice(spans, (0, 0, x, 0), (4, 4, 1, 2)).reshape(32)
    swap = [(0, 1), (1, 0)]
    weight_other = lax.ppermute(out_weight, "c", swap)
    kv = jnp.concatenate((keys, values), axis=1)
    kv = copies(kv, "zh")
    rows = kv.shape[0] * kv.shape[1]
    all_queries = copies(queries, "x")
    kv = copies(kv.reshape(rows, kv.shape[2]), "y")
    kv = kv.reshape(kv.shape[0] * rows, kv.shape[2])
    parts = attend(qspans, kspans, all_queries, kv)
    parts = lax.all_to_all(parts, "x", 0, 0, tiled=True)
    attended = combine(parts)
    attended_other = lax.ppermute(attended, "c", swap)
    partial_sums = project(core.reshape(1), attended, attended_other, out_weight, weight_other)
    share = lax.all_to_all(partial_sums, "zl", 0, 0, tiled=True)
    projected = jnp.sum(share.astype(jnp.float32), axis=0)
    hidden = (residual.astype(jnp.float32) + projected).astype(jnp.bfloat16)
    hidden_f = hidden.astype(jnp.float32)
    squares = copies(jnp.sum(hidden_f * hidden_f, axis=1)[None, :], ("zl", "c"))
    squares = jnp.sum(squares, axis=(0, 1))
    factor = lax.rsqrt(squares / D + EPSILON)
    normed = hidden_f * factor[:, None] * norm_gain.astype(jnp.float32)[None, :]
    return normed.astype(jnp.bfloat16)


def solution(mesh):
    fine = Mesh(mesh.devices.reshape(4, 4, 4, 4, 2), ("y", "zh", "x", "zl", "c"))
    ctx, tp = ("y", "zh", "x"), ("zl", "c")
    return jax.shard_map(
        per_device,
        mesh=fine,
        in_specs=(P(ctx, tp), P(ctx, tp), P(ctx, tp), P(tp, None), P(ctx, tp), P(tp), P()),
        out_specs=P(ctx, tp),
        check_vma=False,
    )
```

time: 246 us -> 141 us (0.57)
  waiting for transfers between devices: 151 us -> 23.1 us
  matrix products: 28.2 us -> 0 us
  starting transfers between devices: 4.25 us -> 32.1 us
  blocking collectives: 29.9 us -> 56.9 us
  Pallas kernels: 0 us -> 20 us
  between operations: 13.5 us -> 0.08 us
  other arithmetic: 10.6 us -> 1.75 us
    all_gather x1 -> x0, waiting for transfers between devices: 146 us -> none  [side_by_side(): lax.all_gather(both, axis, axis=dim, tiled=True)]
    dot_general x17 -> x0, matrix products: 28.2 us -> none  [the longest x8 14.1 us: scan_step(): jnp.einsum('hgqk,khd->hgqd', weights.astype(jnp.bfloat16), value_mat, pre...]
    all_to_all x1 -> x3, blocking collectives: 29.9 us -> 56.9 us  [the longest x1 23 us: copies(): lax.all_to_all(stacked, axis, split_axis=0, concat_axis=0, tiled=True)]
    pallas_call x0 -> x3, Pallas kernels: none -> 20 us  [the longest x1 13.2 us: attend(): pl.pallas_call(attention_kernel, out_shape=jax.ShapeDtypeStruct((peers, l...]
    ppermute x0 -> x2, starting transfers between devices: none -> 19.9 us  [the longest x1 11 us: per_device(): attended_other = lax.ppermute(attended, 'c', swap)]
    all_to_all x1 -> x3, waiting for transfers between devices: 4.84 us -> 21.9 us  [copies(): lax.all_to_all(stacked, axis, split_axis=0, concat_axis=0, tiled=True)]
    all_to_all x1 -> x3, starting transfers between devices: 4.25 us -> 12.3 us  [copies(): lax.all_to_all(stacked, axis, split_axis=0, concat_axis=0, tiled=True)]
    split x1 -> x0, local copies, waits for them, and re-layouts: 4.46 us -> none  [side_by_side(): jnp.split(lax.all_gather(both, axis, axis=dim, tiled=True), ends, axis=al...]
  transfers between devices with their start and end apart: 2 -> 5, of which waited for: 2 -> 4; matrix products, arithmetic and copies ran while one was open for 1% -> 4% of each run, Pallas kernels for 0% -> 11%
where the time goes in v1:
time: 141 us; the launch traced here: 140 us
  blocking collectives  56.9 us (40%)
  starting transfers between devices  32.1 us (23%)
  waiting for transfers between devices  23.1 us (16%)
  Pallas kernels  20 us (14%)
  local copies, waits for them, and re-layouts  6.47 us (5%)
  other arithmetic  1.75 us (1%)
    all_to_all x1, blocking collectives, copies(): lax.all_to_all(stacked, axis, split_axis=0, concat_axis=0, tiled=True)  23 us
    all_to_all x1, blocking collectives, per_device(): share = lax.all_to_all(partial_sums, 'zl', 0, 0, tiled=True)  22.4 us
    all_to_all x3, waiting for transfers between devices, copies(): lax.all_to_all(stacked, axis, split_axis=0, concat_axis=0, tiled=True)  21.9 us
    pallas_call x1, Pallas kernels, attend(): pl.pallas_call(attention_kernel, out_shape=jax.ShapeDtypeStruct((peers, l...  13.2 us
    all_to_all x3, starting transfers between devices, copies(): lax.all_to_all(stacked, axis, split_axis=0, concat_axis=0, tiled=True)  12.3 us
    all_to_all x1, blocking collectives, per_device(): parts = lax.all_to_all(parts, 'x', 0, 0, tiled=True)  11.5 us
    ppermute x1, starting transfers between devices, per_device(): attended_other = lax.ppermute(attended, 'c', swap)  11 us
    ppermute x1, starting transfers between devices, per_device(): weight_other = lax.ppermute(out_weight, 'c', swap)  8.87 us
  transfers between devices with their start and end apart: 5, of which 4 were waited for; matrix products, arithmetic and copies ran while one was open for 4% of the time, Pallas kernels for 11%

profile of v1, /device:TPU:1, one launch (start us, length us, event | category | flops | bytes accessed | tf_op | source)
XLA Modules:
  0.0 140.4 jit_solution(12201908595617672353)
XLA Ops:
  0.0 0.0 copy-start.5
  0.0 8.9 %collective-permute-start.1 = (bf16[512,4096]{1,0:T(8,128)(2,1)}, bf16[512,4096]{1,0:T(8,128)(2,1)}, u32[]{:S(2)}, u32[]{:S(2)}) collective-permute-start(bf16[512,4096]{1,0:T(8,128)(2,1)} %w_ref.1), channel_id=1, source_target_pairs={{0,1},{1,0},{2,3},{3,2},{4,5},{5,4},{6,7},{7,6},{8,9},{9,8},{10,11... | collective-permute-start | bytes 12582920 | tf_op jit(solution)/shard_map/ppermute | solution.py:168
  8.9 1.7 %broadcast_in_dim.15 = bf16[4,128,512]{2,1,0:T(8,128)(2,1)} broadcast(bf16[128,512]{1,0:T(8,128)(2,1)} %param.7), dimensions={1,2} | broadcast | bytes 655360 | tf_op jit(solution)/shard_map/broadcast_in_dim | solution.py:23
  10.6 3.5 %all-to-all-start = ((bf16[4,128,512]{2,1,0:T(8,128)(2,1)}), bf16[4,128,512]{2,1,0:T(8,128)(2,1)S(1)}, u32[]{:S(2)}, u32[]{:S(2)}) async-start(bf16[4,128,512]{2,1,0:T(8,128)(2,1)} %broadcast_in_dim.15), calls=%async_computation | async-start | bytes 1048576 | tf_op jit(solution)/shard_map/all_to_all | solution.py:24
  14.1 0.8 pad_maximum_fusion
  14.9 8.7 %all-to-all-done.q_ref = bf16[4,128,512]{2,1,0:T(8,128)(2,1)S(1)} async-done(((bf16[4,128,512]{2,1,0:T(8,128)(2,1)}), bf16[4,128,512]{2,1,0:T(8,128)(2,1)S(1)}, u32[]{:S(2)}, u32[]{:S(2)}) %all-to-all-start) | async-done | bytes 524320 | tf_op jit(solution)/shard_map/all_to_all | solution.py:24
  23.6 0.0 copy-start.1
  23.6 23.0 %all_to_all.30 = bf16[4,128,256]{2,1,0:T(8,128)(2,1)S(1)} all-to-all(bf16[4,128,256]{2,1,0:T(8,128)(2,1)S(1)} %broadcast_in_dim.16), channel_id=1, replica_groups=mesh['y'=4,'zh'=4,'x'=4,'zl'=4,'c'=2] {'zh'}, dimensions={0} | all-to-all | bytes 524288 | tf_op jit(solution)/shard_map/all_to_all | solution.py:24
  46.6 1.0 broadcast_in_dim.17
  47.7 4.2 %all-to-all-start.2 = ((bf16[4,512,256]{2,1,0:T(8,128)(2,1)}), bf16[4,512,256]{2,1,0:T(8,128)(2,1)S(1)}, u32[]{:S(2)}, u32[]{:S(2)}) async-start(bf16[4,512,256]{2,1,0:T(8,128)(2,1)} %broadcast_in_dim.17), calls=%async_computation.2 | async-start | bytes 2097152 | tf_op jit(solution)/shard_map/all_to_all | solution.py:24
  51.9 0.0 copy-done.5
  51.9 0.2 reshape.25
  52.0 0.6 reshape.26.qspan_ref
  52.7 0.6 reshape.27.kspan_ref
  53.3 8.3 %all-to-all-done.2 = bf16[4,512,256]{2,1,0:T(8,128)(2,1)S(1)} async-done(((bf16[4,512,256]{2,1,0:T(8,128)(2,1)}), bf16[4,512,256]{2,1,0:T(8,128)(2,1)S(1)}, u32[]{:S(2)}, u32[]{:S(2)}) %all-to-all-start.2) | async-done | bytes 1048608 | tf_op jit(solution)/shard_map/all_to_all | solution.py:24
  61.6 0.0 copy-start
  61.6 0.0 copy-done.1
  61.6 1.0 copy-done
  62.6 13.2 %attend.1 = bf16[4,144,512]{2,1,0:T(8,128)(2,1)} custom-call(s32[8]{0:T(128)} %reshape.26.qspan_ref, s32[32]{0:T(128)} %reshape.27.kspan_ref, bf16[4,128,512]{2,1,0:T(8,128)(2,1)} %copy-done.1, bf16[2048,256]{1,0:T(8,128)(2,1)} %bitcast.4), custom_call_target="tpu_custom_call" | custom-call | tf_op jit(solution)/shard_map/attend/pallas_call | solution.py:85
  75.8 11.5 %all_to_all.31.p_ref = bf16[4,144,512]{2,1,0:T(8,128)(2,1)} all-to-all(bf16[4,144,512]{2,1,0:T(8,128)(2,1)} %attend.1), channel_id=1, replica_groups=mesh['y'=4,'zh'=4,'x'=4,'zl'=4,'c'=2] {'x'}, dimensions={0} | all-to-all | bytes 1179648 | tf_op jit(solution)/shard_map/all_to_all | solution.py:176
  87.3 2.2 %combine.1.own_ref = bf16[128,512]{1,0:T(8,128)(2,1)} custom-call(bf16[4,144,512]{2,1,0:T(8,128)(2,1)} %all_to_all.31.p_ref), custom_call_target="tpu_custom_call" | custom-call | tf_op jit(solution)/shard_map/combine/pallas_call | solution.py:122
  89.5 11.0 %collective-permute-start = (bf16[128,512]{1,0:T(8,128)(2,1)}, bf16[128,512]{1,0:T(8,128)(2,1)S(1)}, u32[]{:S(2)}, u32[]{:S(2)}) collective-permute-start(bf16[128,512]{1,0:T(8,128)(2,1)} %combine.1.own_ref), channel_id=1, source_target_pairs={{0,1},{1,0},{2,3},{3,2},{4,5},{5,4},{6,7},{7,6},{8,9},{9,8},{10,11... | collective-permute-start | bytes 393224 | tf_op jit(solution)/shard_map/ppermute | solution.py:178
  100.6 1.2 collective-permute-done.other_ref
  101.7 0.0 copy-start.3
  101.7 0.0 collective-permute-done.1.w2_ref
  101.7 0.7 copy-done.3
  102.4 0.0 copy-start.2
  102.4 0.0 copy-start.4
  102.4 4.5 %project.1 = bf16[4,128,512]{2,1,0:T(8,128)(2,1)} custom-call(s32[1]{0:T(128)} %bitcast.core_ref, bf16[128,512]{1,0:T(8,128)(2,1)} %combine.1.own_ref, bf16[128,512]{1,0:T(8,128)(2,1)} %copy-done.3, bf16[512,4096]{1,0:T(8,128)(2,1)} %w_ref.1, bf16[512,4096]{1,0:T(8,128)(2,1)} %collective-permute-done.1.w2_ref), custom_call_target="tpu_custom_call" | custom-call | tf_op jit(solution)/shard_map/project/pallas_call | solution.py:141
  106.9 22.4 %all_to_all.32 = bf16[4,128,512]{2,1,0:T(8,128)(2,1)S(1)} all-to-all(bf16[4,128,512]{2,1,0:T(8,128)(2,1)} %project.1), channel_id=1, replica_groups=mesh['y'=4,'zh'=4,'x'=4,'zl'=4,'c'=2] {'zl'}, dimensions={0} | all-to-all | bytes 1048576 | tf_op jit(solution)/shard_map/all_to_all | solution.py:180
  129.3 0.1 convert_reduce_fusion
  129.4 0.0 copy-done.2
  129.4 0.1 fusion
  129.5 0.6 broadcast_in_dim.18
  130.1 4.6 %all-to-all-start.5 = ((f32[8,1,128]{2,1,0:T(1,128)}), f32[8,1,128]{2,1,0:T(1,128)S(1)}, u32[]{:S(2)}, u32[]{:S(2)}) async-start(f32[8,1,128]{2,1,0:T(1,128)} %broadcast_in_dim.18), calls=%async_computation.5 | async-start | bytes 8192 | tf_op jit(solution)/shard_map/all_to_all | solution.py:24
  134.8 0.0 copy-done.4
  134.8 4.8 %all-to-all-done.5 = f32[8,1,128]{2,1,0:T(1,128)S(1)} async-done(((f32[8,1,128]{2,1,0:T(1,128)}), f32[8,1,128]{2,1,0:T(1,128)S(1)}, u32[]{:S(2)}, u32[]{:S(2)}) %all-to-all-start.5) | async-done | bytes 4128 | tf_op jit(solution)/shard_map/all_to_all | solution.py:24
  139.6 0.8 fusion.2
  (6 shorter events, 0.1 us)
Async XLA Ops:
  0.0 51.9 %copy-start.5 = (s32[128]{0:T(128)S(1)}, s32[128]{0:T(128)}, u32[]{:S(2)}) copy-start(s32[128]{0:T(128)} %param.13) | copy-start | bytes 1540
  0.0 101.7 %collective-permute-start.1 = (bf16[512,4096]{1,0:T(8,128)(2,1)}, bf16[512,4096]{1,0:T(8,128)(2,1)}, u32[]{:S(2)}, u32[]{:S(2)}) collective-permute-start(bf16[512,4096]{1,0:T(8,128)(2,1)} %w_ref.1), channel_id=1, source_target_pairs={{0,1},{1,0},{2,3},{3,2},{4,5},{5,4},{6,7},{7,6},{8,9},{9,8},{10,11... | collective-permute-start | bytes 12582920 | tf_op jit(solution)/shard_map/ppermute | solution.py:168
  10.6 13.0 %all-to-all-start = ((bf16[4,128,512]{2,1,0:T(8,128)(2,1)}), bf16[4,128,512]{2,1,0:T(8,128)(2,1)S(1)}, u32[]{:S(2)}, u32[]{:S(2)}) async-start(bf16[4,128,512]{2,1,0:T(8,128)(2,1)} %broadcast_in_dim.15), calls=%async_computation | async-start | bytes 1048576 | tf_op jit(solution)/shard_map/all_to_all | solution.py:24
  23.6 38.0 %copy-start.1 = (bf16[4,128,512]{2,1,0:T(8,128)(2,1)}, bf16[4,128,512]{2,1,0:T(8,128)(2,1)S(1)}, u32[]{:S(2)}) copy-start(bf16[4,128,512]{2,1,0:T(8,128)(2,1)S(1)} %all-to-all-done.q_ref) | copy-start | bytes 1572868
  47.7 13.9 %all-to-all-start.2 = ((bf16[4,512,256]{2,1,0:T(8,128)(2,1)}), bf16[4,512,256]{2,1,0:T(8,128)(2,1)S(1)}, u32[]{:S(2)}, u32[]{:S(2)}) async-start(bf16[4,512,256]{2,1,0:T(8,128)(2,1)} %broadcast_in_dim.17), calls=%async_computation.2 | async-start | bytes 2097152 | tf_op jit(solution)/shard_map/all_to_all | solution.py:24
  61.6 1.0 copy-start
  89.5 12.2 %collective-permute-start = (bf16[128,512]{1,0:T(8,128)(2,1)}, bf16[128,512]{1,0:T(8,128)(2,1)S(1)}, u32[]{:S(2)}, u32[]{:S(2)}) collective-permute-start(bf16[128,512]{1,0:T(8,128)(2,1)} %combine.1.own_ref), channel_id=1, source_target_pairs={{0,1},{1,0},{2,3},{3,2},{4,5},{5,4},{6,7},{7,6},{8,9},{9,8},{10,11... | collective-permute-start | bytes 393224 | tf_op jit(solution)/shard_map/ppermute | solution.py:178
  101.7 0.7 copy-start.3
  102.4 27.0 %copy-start.2 = (bf16[128,512]{1,0:T(8,128)(2,1)S(1)}, bf16[128,512]{1,0:T(8,128)(2,1)}, u32[]{:S(2)}) copy-start(bf16[128,512]{1,0:T(8,128)(2,1)} %param.11) | copy-start | bytes 393220
  102.4 32.4 %copy-start.4 = (bf16[512]{0:T(512)(128)(2,1)S(1)}, bf16[512]{0:T(512)(128)(2,1)}, u32[]{:S(2)}) copy-start(bf16[512]{0:T(512)(128)(2,1)} %param.12) | copy-start | bytes 3076
  130.1 9.5 %all-to-all-start.5 = ((f32[8,1,128]{2,1,0:T(1,128)}), f32[8,1,128]{2,1,0:T(1,128)S(1)}, u32[]{:S(2)}, u32[]{:S(2)}) async-start(f32[8,1,128]{2,1,0:T(1,128)} %broadcast_in_dim.18), calls=%async_computation.5 | async-start | bytes 8192 | tf_op jit(solution)/shard_map/all_to_all | solution.py:24

commit v2 on v1

--- a/solution.py
+++ b/solution.py
@@ -7,6 +7,7 @@
 from jax.experimental import pallas as pl
 from jax.experimental.pallas import tpu as pltpu
 from jax.sharding import Mesh, PartitionSpec as P
+
 
 D = 4096
 HEAD_SIZE = 128
@@ -24,75 +25,160 @@
     return lax.all_to_all(stacked, axis, split_axis=0, concat_axis=0, tiled=True)
 
 
-def attention_kernel(qspan_ref, kspan_ref, q_ref, kv_ref, o_ref, vt_ref, s_ref):
+def plan_kernel(dev_ref, span_ref, o_ref, flag_ref):
+    dev = dev_ref[0]
+    x = dev & 3
+    row = dev >> 2
+    n_spans = span_ref.shape[0]
+    n_keys = n_spans // 4
+
+    def clear(i, c):
+        flag_ref[i] = -1
+        return c
+
+    lax.fori_loop(0, n_spans, clear, 0, unroll=16)
+
+    def mark(i, c):
+        slot = ((i >> 1) * 4 + x) * 2 + (i & 1)
+        flag_ref[span_ref[slot]] = i
+        return c
+
+    lax.fori_loop(0, n_keys, mark, 0, unroll=8)
+
+    def walk(p, n):
+        f = flag_ref[p]
+        o_ref[64 + n] = p
+        o_ref[128 + n] = f
+        n = n + jnp.where(f >= 0, 1, 0)
+        flag_ref[p] = n
+        return n
+
+    lax.fori_loop(0, n_spans, walk, 0, unroll=8)
+    for t in range(8):
+        peer = (x + t // 2) & 3
+        span = span_ref[(row * 4 + peer) * 2 + t % 2]
+        o_ref[t] = span
+        o_ref[8 + t] = jnp.maximum((flag_ref[span] + 3) >> 2, 1)
+        if t % 2 == 0:
+            o_ref[16 + t // 2] = peer
+
+
+def plan(dev, span_order):
+    smem = pl.BlockSpec(memory_space=pltpu.SMEM)
+    return pl.pallas_call(
+        plan_kernel,
+        out_shape=jax.ShapeDtypeStruct((256,), jnp.int32),
+        in_specs=[smem, smem],
+        out_specs=smem,
+        scratch_shapes=[pltpu.SMEM((128,), jnp.int32)],
+        name="plan",
+    )(dev, span_order)
+
+
+def attention_kernel(tab_ref, q0_ref, q1_ref, q2_ref, q3_ref, kv_ref, o_ref, k_ref, v_ref, q_ref, s_ref, mx_ref, l_ref, acc_ref):
+    rows = HEADS * SPAN
+    block = 4 * SPAN
+    lanes = HEAD_SIZE
     n_keys = kv_ref.shape[0]
+    for i in range(n_keys // SPAN):
+        src = pl.multiple_of(tab_ref[128 + i] * SPAN, SPAN)
+        k_ref[i * SPAN : (i + 1) * SPAN, :] = kv_ref[pl.ds(src, SPAN), :HEAD_SIZE]
+        v_ref[i * SPAN : (i + 1) * SPAN, :] = kv_ref[pl.ds(src, SPAN), HEAD_SIZE:]
+    q_refs = (q0_ref, q1_ref, q2_ref, q3_ref)
+    for peer in range(4):
+        for half in range(2):
+            for h in range(HEADS):
+                at = ((peer * 2 + half) * HEADS + h) * SPAN
+                q_ref[at : at + SPAN, :] = q_refs[peer][
+                    half * SPAN : (half + 1) * SPAN, h * HEAD_SIZE : (h + 1) * HEAD_SIZE
+                ]
+    lane = lax.broadcasted_iota(jnp.int32, (rows, block), 1)
+    diff = (lane % SPAN) - (lax.broadcasted_iota(jnp.int32, (rows, block), 0) % SPAN)
+    lane_row = lax.broadcasted_iota(jnp.int32, (1, block), 1) // SPAN
+    rest = n_keys // block - 1
+
+    def pair(peer, mx_ref, l_ref, acc_ref, s_ref):
+        nb = [tab_ref[8 + 2 * peer + half] for half in range(2)]
+        work = [(0, nb[0] - 1), (1, nb[1] - 1)]
+        for j in range(rest):
+            second = j - (nb[0] - 1)
+            half = jnp.where(second < 0, 0, jnp.where(second < nb[1] - 1, 1, 2))
+            work.append((half, jnp.where(second < 0, j, jnp.where(second < nb[1] - 1, second, 0))))
+        mx_ref[2] = jnp.zeros((rows, lanes), jnp.float32)
+        for b, (half, kb) in enumerate(work):
+            q_half = half if b < 2 else jnp.minimum(half, 1)
+            q = q_ref[pl.ds(pl.multiple_of((peer * 2 + q_half) * rows, rows), rows), :]
+            k = k_ref[pl.ds(pl.multiple_of(kb * block, block), block), :]
+            s = lax.dot_general(q, k, (((1,), (1,)), ((), ())), preferred_element_type=jnp.float32)
+            if b < 2:
+                qspan = tab_ref[2 * peer + half]
+                limits = [(qspan - tab_ref[64 + 4 * kb + j]) * SPAN for j in range(4)]
+                limit = jnp.full((1, block), limits[0], jnp.int32)
+                for j in range(1, 4):
+                    limit = jnp.where(lane_row >= j, limits[j], limit)
+                s = jnp.where(diff <= limit, s, NEG)
+            s_ref[b] = s
+            top = jnp.maximum(s[:, :lanes], s[:, lanes:])
+            mx_ref[half] = top if b < 2 else jnp.maximum(mx_ref[half], top)
+        for half in range(2):
+            mx_ref[half] = jnp.broadcast_to(jnp.max(mx_ref[half], axis=1, keepdims=True), (rows, lanes))
+        for b, (half, kb) in enumerate(work):
+            m = mx_ref[half]
+            s = s_ref[b]
+            w0 = jnp.exp2((s[:, :lanes] - m) * (SCALE * LOG2E))
+            w1 = jnp.exp2((s[:, lanes:] - m) * (SCALE * LOG2E))
+            v = v_ref[pl.ds(pl.multiple_of(kb * block, block), block), :]
+            w = jnp.concatenate([w0.astype(jnp.bfloat16), w1.astype(jnp.bfloat16)], axis=1)
+            out = jnp.dot(w, v, preferred_element_type=jnp.float32)
+            if b < 2:
+                l_ref[half] = w0 + w1
+                acc_ref[half] = out
+            else:
+                l_ref[half] = l_ref[half] + (w0 + w1)
+                acc_ref[half] = acc_ref[half] + out
+        dest = tab_ref[16 + peer]
+        which = lax.broadcasted_iota(jnp.int32, (rows, lanes), 1)
+        for half in range(2):
+            total = jnp.broadcast_to(jnp.sum(l_ref[half], axis=1, keepdims=True), (rows, lanes))
+            out = (acc_ref[half] * (1.0 / total)).astype(jnp.bfloat16)
+            for h in range(HEADS):
+                o_ref[dest, half * SPAN : (half + 1) * SPAN, h * HEAD_SIZE : (h + 1) * HEAD_SIZE] = out[
+                    h * SPAN : (h + 1) * SPAN
+                ]
+            lse = mx_ref[half] * SCALE + jnp.log(total)
+            hi = lse.astype(jnp.bfloat16).astype(jnp.float32)
+            mid = (lse - hi).astype(jnp.bfloat16).astype(jnp.float32)
+            low = lse - hi - mid
+            stats = jnp.where(which == 0, hi, jnp.where(which == 1, mid, jnp.where(which == 2, low, 0.0)))
+            o_ref[dest, 2 * SPAN :, half * rows : (half + 1) * rows] = stats.T[:STAT_ROWS].astype(jnp.bfloat16)
+
+    for peer in range(4):
+        pair(peer, mx_ref.at[peer], l_ref.at[peer], acc_ref.at[peer], s_ref.at[peer])
+
+
+def attend(table, queries, kv):
+    local, width = queries[0].shape
+    peers = len(queries)
+    n_keys = kv.shape[0]
     rows = HEADS * SPAN
-    block = 256
-    vt_ref[...] = kv_ref[:, HEAD_SIZE:].T
-    diff = lax.broadcasted_iota(jnp.int32, (SPAN, rows), 0) - (
-        lax.broadcasted_iota(jnp.int32, (SPAN, rows), 1) % SPAN
-    )
-
-    def tile(t, carry):
-        peer = t // 2
-        half = t % 2
-        row0 = pl.multiple_of(half * SPAN, SPAN)
-        qspan = qspan_ref[t]
-        q = jnp.concatenate(
-            [q_ref[peer, pl.ds(row0, SPAN), h * HEAD_SIZE : (h + 1) * HEAD_SIZE] for h in range(HEADS)],
-            axis=0,
-        )
-        top = jnp.full((1, rows), NEG, jnp.float32)
-        for b in range(n_keys // block):
-            k = kv_ref[b * block : (b + 1) * block, :HEAD_SIZE]
-            s = lax.dot_general(k, q, (((1,), (1,)), ((), ())), preferred_element_type=jnp.float32)
-            for j in range(block // SPAN):
-                n = b * (block // SPAN) + j
-                limit = (qspan - kspan_ref[n]) * SPAN
-                piece = jnp.where(diff <= limit, s[j * SPAN : (j + 1) * SPAN], NEG)
-                s_ref[n * SPAN : (n + 1) * SPAN, :] = piece
-                top = jnp.maximum(top, jnp.max(piece, axis=0, keepdims=True))
-        total = jnp.zeros((1, rows), jnp.float32)
-        acc = jnp.zeros((HEAD_SIZE, rows), jnp.float32)
-        for b in range(n_keys // block):
-            w = jnp.exp2((s_ref[b * block : (b + 1) * block, :] - top) * (SCALE * LOG2E))
-            total = total + jnp.sum(w, axis=0, keepdims=True)
-            acc = acc + jnp.dot(
-                vt_ref[:, b * block : (b + 1) * block],
-                w.astype(jnp.bfloat16),
-                preferred_element_type=jnp.float32,
-            )
-        out = (acc / total).T.astype(jnp.bfloat16)
-        for h in range(HEADS):
-            o_ref[peer, pl.ds(row0, SPAN), h * HEAD_SIZE : (h + 1) * HEAD_SIZE] = out[h * SPAN : (h + 1) * SPAN]
-        lse = top * SCALE + jnp.log(total)
-        hi = lse.astype(jnp.bfloat16).astype(jnp.float32)
-        mid = (lse - hi).astype(jnp.bfloat16).astype(jnp.float32)
-        low = lse - hi - mid
-        stats = jnp.concatenate([hi, mid, low, jnp.zeros((STAT_ROWS - 3, rows), jnp.float32)], axis=0)
-        col0 = pl.multiple_of(half * rows, rows)
-        o_ref[peer, 2 * SPAN :, pl.ds(col0, rows)] = stats.astype(jnp.bfloat16)
-        return carry
-
-    lax.fori_loop(0, 2 * q_ref.shape[0], tile, 0)
-
-
-def attend(qspans, kspans, queries, kv):
-    peers, local, width = queries.shape
-    n_keys = kv.shape[0]
     vmem = pl.BlockSpec(memory_space=pltpu.VMEM)
     smem = pl.BlockSpec(memory_space=pltpu.SMEM)
     return pl.pallas_call(
         attention_kernel,
         out_shape=jax.ShapeDtypeStruct((peers, local + STAT_ROWS, width), jnp.bfloat16),
-        in_specs=[smem, smem, vmem, vmem],
+        in_specs=[smem] + [vmem] * (peers + 1),
         out_specs=vmem,
         scratch_shapes=[
-            pltpu.VMEM((HEAD_SIZE, n_keys), jnp.bfloat16),
-            pltpu.VMEM((n_keys, HEADS * SPAN), jnp.float32),
+            pltpu.VMEM((n_keys, HEAD_SIZE), jnp.bfloat16),
+            pltpu.VMEM((n_keys, HEAD_SIZE), jnp.bfloat16),
+            pltpu.VMEM((peers * 2 * rows, HEAD_SIZE), jnp.bfloat16),
+            pltpu.VMEM((peers, n_keys // rows + 1, rows, rows), jnp.float32),
+            pltpu.VMEM((peers, 3, rows, HEAD_SIZE), jnp.float32),
+            pltpu.VMEM((peers, 3, rows, HEAD_SIZE), jnp.float32),
+            pltpu.VMEM((peers, 3, rows, HEAD_SIZE), jnp.float32),
         ],
         name="attend",
-    )(qspans, kspans, queries, kv)
+    )(table, *queries, kv)
 
 
 def combine_kernel(p_ref, o_ref):
@@ -117,7 +203,7 @@
 
 
 def combine(parts):
-    peers, local, width = parts.shape
+    _, _, width = parts.shape
     vmem = pl.BlockSpec(memory_space=pltpu.VMEM)
     return pl.pallas_call(
         combine_kernel,
@@ -161,18 +247,15 @@
     zh = lax.axis_index("zh")
     x = lax.axis_index("x")
     core = lax.axis_index("c")
-    spans = span_order.reshape(4, 4, 4, 2)
-    qspans = lax.dynamic_slice(spans, (y, zh, 0, 0), (1, 1, 4, 2)).reshape(8)
-    kspans = lax.dynamic_slice(spans, (0, 0, x, 0), (4, 4, 1, 2)).reshape(32)
     swap = [(0, 1), (1, 0)]
+    kv = copies(jnp.concatenate((keys, values), axis=1), "zh")
+    rows = kv.shape[0] * kv.shape[1]
+    qs = [queries] + [lax.ppermute(queries, "x", [(i, (i - d) % 4) for i in range(4)]) for d in (1, 2, 3)]
     weight_other = lax.ppermute(out_weight, "c", swap)
-    kv = jnp.concatenate((keys, values), axis=1)
-    kv = copies(kv, "zh")
-    rows = kv.shape[0] * kv.shape[1]
-    all_queries = copies(queries, "x")
     kv = copies(kv.reshape(rows, kv.shape[2]), "y")
+    table = plan(((y * 4 + zh) * 4 + x).reshape(1), span_order)
     kv = kv.reshape(kv.shape[0] * rows, kv.shape[2])
-    parts = attend(qspans, kspans, all_queries, kv)
+    parts = attend(table, qs, kv)
     parts = lax.all_to_all(parts, "x", 0, 0, tiled=True)
     attended = combine(parts)
     attended_other = lax.ppermute(attended, "c", swap)

time: 141 us -> 125 us (0.89)
  waiting for transfers between devices: 23.1 us -> 8.42 us
  starting transfers between devices: 32.1 us -> 36.8 us
  local copies, waits for them, and re-layouts: 6.47 us -> 3.31 us
  Pallas kernels: 20 us -> 18.2 us
    all_to_all x3 -> x2, waiting for transfers between devices: 21.9 us -> 4.84 us  [copies(): lax.all_to_all(stacked, axis, split_axis=0, concat_axis=0, tiled=True)]
    ppermute x0 -> x3, starting transfers between devices: none -> 9.32 us  [per_device(): lax.ppermute(queries, 'x', [(i, (i - d) % 4) for i in range(4)])]
    pallas_call x1, Pallas kernels: 13.2 us -> 9.21 us  [attend(): pl.pallas_call(attention_kernel, out_shape=jax.ShapeDtypeStruct((peers, l...]
    all_to_all x3 -> x2, starting transfers between devices: 12.3 us -> 8.79 us  [copies(): lax.all_to_all(stacked, axis, split_axis=0, concat_axis=0, tiled=True)]
    ppermute x0 -> x3, waiting for transfers between devices: none -> 2.41 us  [per_device(): lax.ppermute(queries, 'x', [(i, (i - d) % 4) for i in range(4)])]
    pallas_call x0 -> x1, Pallas kernels: none -> 2.23 us  [plan(): pl.pallas_call(plan_kernel, out_shape=jax.ShapeDtypeStruct((256,), jnp.in...]
    all_to_all x1, blocking collectives: 22.4 us -> 20.4 us  [per_device(): share = lax.all_to_all(partial_sums, 'zl', 0, 0, tiled=True)]
    broadcast_in_dim x4 -> x3, local copies, waits for them, and re-layouts: 3.4 us -> 1.65 us  [copies(): stacked = jnp.broadcast_to(shard, (lax.axis_size(axis), *shard.shape))]
  transfers between devices with their start and end apart: 5 -> 7, of which waited for: 4 -> 3; matrix products, arithmetic and copies ran while one was open for 4% -> 1% of each run, Pallas kernels for 11% -> 11%
where the time goes in v2:
time: 125 us; the launch traced here: 124 us
  blocking collectives  55.5 us (44%)
  starting transfers between devices  36.8 us (29%)
  Pallas kernels  18.2 us (15%)
  waiting for transfers between devices  8.42 us (7%)
  local copies, waits for them, and re-layouts  3.31 us (3%)
  other arithmetic  1.75 us (1%)
    all_to_all x1, blocking collectives, copies(): lax.all_to_all(stacked, axis, split_axis=0, concat_axis=0, tiled=True)  23.6 us
    all_to_all x1, blocking collectives, per_device(): share = lax.all_to_all(partial_sums, 'zl', 0, 0, tiled=True)  20.4 us
    all_to_all x1, blocking collectives, per_device(): parts = lax.all_to_all(parts, 'x', 0, 0, tiled=True)  11.5 us
    ppermute x1, starting transfers between devices, per_device(): attended_other = lax.ppermute(attended, 'c', swap)  9.87 us
    ppermute x3, starting transfers between devices, per_device(): lax.ppermute(queries, 'x', [(i, (i - d) % 4) for i in range(4)])  9.32 us
    pallas_call x1, Pallas kernels, attend(): pl.pallas_call(attention_kernel, out_shape=jax.ShapeDtypeStruct((peers, l...  9.21 us
    ppermute x1, starting transfers between devices, per_device(): weight_other = lax.ppermute(out_weight, 'c', swap)  8.87 us
    all_to_all x2, starting transfers between devices, copies(): lax.all_to_all(stacked, axis, split_axis=0, concat_axis=0, tiled=True)  8.79 us
  transfers between devices with their start and end apart: 7, of which 3 were waited for; matrix products, arithmetic and copies ran while one was open for 1% of the time, Pallas kernels for 11%

profile of v2, /device:TPU:1, one launch (start us, length us, event | category | flops | bytes accessed | tf_op | source)
XLA Modules:
  0.0 124.2 jit_solution(3965686885697795928)
XLA Ops:
  0.0 0.0 copy-start.3
  0.0 8.9 %collective-permute-start.4 = (bf16[512,4096]{1,0:T(8,128)(2,1)}, bf16[512,4096]{1,0:T(8,128)(2,1)}, u32[]{:S(2)}, u32[]{:S(2)}) collective-permute-start(bf16[512,4096]{1,0:T(8,128)(2,1)} %w_ref.1), channel_id=1, source_target_pairs={{0,1},{1,0},{2,3},{3,2},{4,5},{5,4},{6,7},{7,6},{8,9},{9,8},{10,11... | collective-permute-start | bytes 12582920 | tf_op jit(solution)/shard_map/ppermute | solution.py:254
  8.9 0.8 pad_maximum_fusion
  9.7 23.6 %all_to_all.25 = bf16[4,128,256]{2,1,0:T(8,128)(2,1)S(1)} all-to-all(bf16[4,128,256]{2,1,0:T(8,128)(2,1)S(1)} %broadcast_in_dim.12), channel_id=1, replica_groups=mesh['y'=4,'zh'=4,'x'=4,'zl'=4,'c'=2] {'zh'}, dimensions={0} | all-to-all | bytes 524288 | tf_op jit(solution)/shard_map/all_to_all | solution.py:25
  33.3 1.0 broadcast_in_dim.13
  34.3 4.2 %all-to-all-start.1 = ((bf16[4,512,256]{2,1,0:T(8,128)(2,1)}), bf16[4,512,256]{2,1,0:T(8,128)(2,1)S(1)}, u32[]{:S(2)}, u32[]{:S(2)}) async-start(bf16[4,512,256]{2,1,0:T(8,128)(2,1)} %broadcast_in_dim.13), calls=%async_computation.1 | async-start | bytes 2097152 | tf_op jit(solution)/shard_map/all_to_all | solution.py:25
  38.5 0.0 copy-done.3
  38.5 4.4 %collective-permute-start = (bf16[128,512]{1,0:T(8,128)(2,1)S(1)}, bf16[128,512]{1,0:T(8,128)(2,1)S(1)}, u32[]{:S(2)}, u32[]{:S(2)}) collective-permute-start(bf16[128,512]{1,0:T(8,128)(2,1)S(1)} %copy-done.3), channel_id=1, source_target_pairs={{0,24},{8,0},{16,8},{24,16},{1,25},{9,1},{17,9},{25,17},{2,26},{10... | collective-permute-start | bytes 393224 | tf_op jit(solution)/shard_map/ppermute | solution.py:253
  42.9 2.4 %collective-permute-start.1 = (bf16[128,512]{1,0:T(8,128)(2,1)S(1)}, bf16[128,512]{1,0:T(8,128)(2,1)S(1)}, u32[]{:S(2)}, u32[]{:S(2)}) collective-permute-start(bf16[128,512]{1,0:T(8,128)(2,1)S(1)} %copy-done.3), channel_id=1, source_target_pairs={{0,16},{8,24},{16,0},{24,8},{1,17},{9,25},{17,1},{25,9},{2,18},{10... | collective-permute-start | bytes 393224 | tf_op jit(solution)/shard_map/ppermute | solution.py:253
  45.3 2.5 %collective-permute-start.2 = (bf16[128,512]{1,0:T(8,128)(2,1)S(1)}, bf16[128,512]{1,0:T(8,128)(2,1)S(1)}, u32[]{:S(2)}, u32[]{:S(2)}) collective-permute-start(bf16[128,512]{1,0:T(8,128)(2,1)S(1)} %copy-done.3), channel_id=1, source_target_pairs={{0,8},{8,16},{16,24},{24,0},{1,9},{9,17},{17,25},{25,1},{2,10},{10... | collective-permute-start | bytes 393224 | tf_op jit(solution)/shard_map/ppermute | solution.py:253
  47.8 2.2 %plan.1.tab_ref = s32[256]{0:T(256)} custom-call(s32[1]{0:T(128)} %bitcast.1.dev_ref, s32[128]{0:T(128)} %span_ref.1), custom_call_target="tpu_custom_call" | custom-call | tf_op jit(solution)/shard_map/plan/pallas_call | solution.py:68
  50.1 0.0 collective-permute-done.q1_ref
  50.1 0.0 copy-start.4
  50.1 0.0 collective-permute-done.1.q2_ref
  50.1 0.0 copy-start.5
  50.1 2.4 %collective-permute-done.2.q3_ref = bf16[128,512]{1,0:T(8,128)(2,1)S(1)} collective-permute-done((bf16[128,512]{1,0:T(8,128)(2,1)S(1)}, bf16[128,512]{1,0:T(8,128)(2,1)S(1)}, u32[]{:S(2)}, u32[]{:S(2)}) %collective-permute-start.2) | collective-permute-done | bytes 131104 | tf_op jit(solution)/shard_map/ppermute | solution.py:253
  52.5 0.0 copy-start.6
  52.5 0.0 all-to-all-done.1
  52.5 0.0 copy-start
  52.5 0.0 copy-done.4
  52.5 0.0 copy-done.5
  52.5 0.6 copy-done.6
  53.2 0.3 copy-done
  53.5 9.2 %attend.1 = bf16[4,144,512]{2,1,0:T(8,128)(2,1)} custom-call(s32[256]{0:T(256)} %plan.1.tab_ref, bf16[128,512]{1,0:T(8,128)(2,1)} %q0_ref.1, bf16[128,512]{1,0:T(8,128)(2,1)} %copy-done.4, bf16[128,512]{1,0:T(8,128)(2,1)} %copy-done.5, bf16[128,512]{1,0:T(8,128)(2,1)} %copy-done.6, bf16[2048,256]{1,0:T(8,128)(2,1)} %bitcast.5), custom_call_target="tpu_custom_call" | custom-call | tf_op jit(solution)/shard_map/attend/pallas_call | solution.py:166
  62.7 11.5 %all_to_all.26.p_ref = bf16[4,144,512]{2,1,0:T(8,128)(2,1)} all-to-all(bf16[4,144,512]{2,1,0:T(8,128)(2,1)} %attend.1), channel_id=1, replica_groups=mesh['y'=4,'zh'=4,'x'=4,'zl'=4,'c'=2] {'x'}, dimensions={0} | all-to-all | bytes 1179648 | tf_op jit(solution)/shard_map/all_to_all | solution.py:259
  74.2 2.2 %combine.1.own_ref = bf16[128,512]{1,0:T(8,128)(2,1)} custom-call(bf16[4,144,512]{2,1,0:T(8,128)(2,1)} %all_to_all.26.p_ref), custom_call_target="tpu_custom_call" | custom-call | tf_op jit(solution)/shard_map/combine/pallas_call | solution.py:208
  76.5 9.9 %collective-permute-start.3 = (bf16[128,512]{1,0:T(8,128)(2,1)}, bf16[128,512]{1,0:T(8,128)(2,1)S(1)}, u32[]{:S(2)}, u32[]{:S(2)}) collective-permute-start(bf16[128,512]{1,0:T(8,128)(2,1)} %combine.1.own_ref), channel_id=1, source_target_pairs={{0,1},{1,0},{2,3},{3,2},{4,5},{5,4},{6,7},{7,6},{8,9},{9,8},{10,11... | collective-permute-start | bytes 393224 | tf_op jit(solution)/shard_map/ppermute | solution.py:261
  86.3 1.2 collective-permute-done.3.other_ref
  87.5 0.0 copy-start.2
  87.5 0.0 collective-permute-done.4.w2_ref
  87.5 0.7 copy-done.2
  88.2 0.0 copy-start.1
  88.2 0.0 copy-start.7
  88.2 4.5 %project.1 = bf16[4,128,512]{2,1,0:T(8,128)(2,1)} custom-call(s32[1]{0:T(128)} %bitcast.core_ref, bf16[128,512]{1,0:T(8,128)(2,1)} %combine.1.own_ref, bf16[128,512]{1,0:T(8,128)(2,1)} %copy-done.2, bf16[512,4096]{1,0:T(8,128)(2,1)} %w_ref.1, bf16[512,4096]{1,0:T(8,128)(2,1)} %collective-permute-done.4.w2_ref), custom_call_target="tpu_custom_call" | custom-call | tf_op jit(solution)/shard_map/project/pallas_call | solution.py:227
  92.7 20.4 %all_to_all.27 = bf16[4,128,512]{2,1,0:T(8,128)(2,1)S(1)} all-to-all(bf16[4,128,512]{2,1,0:T(8,128)(2,1)} %project.1), channel_id=1, replica_groups=mesh['y'=4,'zh'=4,'x'=4,'zl'=4,'c'=2] {'zl'}, dimensions={0} | all-to-all | bytes 1048576 | tf_op jit(solution)/shard_map/all_to_all | solution.py:263
  113.1 0.1 convert_reduce_fusion
  113.2 0.0 copy-done.1
  113.2 0.1 fusion
  113.3 0.6 broadcast_in_dim.14
  113.9 4.6 %all-to-all-start.4 = ((f32[8,1,128]{2,1,0:T(1,128)}), f32[8,1,128]{2,1,0:T(1,128)S(1)}, u32[]{:S(2)}, u32[]{:S(2)}) async-start(f32[8,1,128]{2,1,0:T(1,128)} %broadcast_in_dim.14), calls=%async_computation.4 | async-start | bytes 8192 | tf_op jit(solution)/shard_map/all_to_all | solution.py:25
  118.5 0.0 copy-done.7
  118.6 4.8 %all-to-all-done.4 = f32[8,1,128]{2,1,0:T(1,128)S(1)} async-done(((f32[8,1,128]{2,1,0:T(1,128)}), f32[8,1,128]{2,1,0:T(1,128)S(1)}, u32[]{:S(2)}, u32[]{:S(2)}) %all-to-all-start.4) | async-done | bytes 4128 | tf_op jit(solution)/shard_map/all_to_all | solution.py:25
  123.4 0.8 fusion.2
  (4 shorter events, 0.0 us)
Async XLA Ops:
  0.0 38.5 %copy-start.3 = (bf16[128,512]{1,0:T(8,128)(2,1)S(1)}, bf16[128,512]{1,0:T(8,128)(2,1)}, u32[]{:S(2)}) copy-start(bf16[128,512]{1,0:T(8,128)(2,1)} %q0_ref.1) | copy-start | bytes 393220
  0.0 87.5 %collective-permute-start.4 = (bf16[512,4096]{1,0:T(8,128)(2,1)}, bf16[512,4096]{1,0:T(8,128)(2,1)}, u32[]{:S(2)}, u32[]{:S(2)}) collective-permute-start(bf16[512,4096]{1,0:T(8,128)(2,1)} %w_ref.1), channel_id=1, source_target_pairs={{0,1},{1,0},{2,3},{3,2},{4,5},{5,4},{6,7},{7,6},{8,9},{9,8},{10,11... | collective-permute-start | bytes 12582920 | tf_op jit(solution)/shard_map/ppermute | solution.py:254
  34.3 18.2 %all-to-all-start.1 = ((bf16[4,512,256]{2,1,0:T(8,128)(2,1)}), bf16[4,512,256]{2,1,0:T(8,128)(2,1)S(1)}, u32[]{:S(2)}, u32[]{:S(2)}) async-start(bf16[4,512,256]{2,1,0:T(8,128)(2,1)} %broadcast_in_dim.13), calls=%async_computation.1 | async-start | bytes 2097152 | tf_op jit(solution)/shard_map/all_to_all | solution.py:25
  38.5 11.6 %collective-permute-start = (bf16[128,512]{1,0:T(8,128)(2,1)S(1)}, bf16[128,512]{1,0:T(8,128)(2,1)S(1)}, u32[]{:S(2)}, u32[]{:S(2)}) collective-permute-start(bf16[128,512]{1,0:T(8,128)(2,1)S(1)} %copy-done.3), channel_id=1, source_target_pairs={{0,24},{8,0},{16,8},{24,16},{1,25},{9,1},{17,9},{25,17},{2,26},{10... | collective-permute-start | bytes 393224 | tf_op jit(solution)/shard_map/ppermute | solution.py:253
  42.9 7.2 %collective-permute-start.1 = (bf16[128,512]{1,0:T(8,128)(2,1)S(1)}, bf16[128,512]{1,0:T(8,128)(2,1)S(1)}, u32[]{:S(2)}, u32[]{:S(2)}) collective-permute-start(bf16[128,512]{1,0:T(8,128)(2,1)S(1)} %copy-done.3), channel_id=1, source_target_pairs={{0,16},{8,24},{16,0},{24,8},{1,17},{9,25},{17,1},{25,9},{2,18},{10... | collective-permute-start | bytes 393224 | tf_op jit(solution)/shard_map/ppermute | solution.py:253
  45.3 7.2 %collective-permute-start.2 = (bf16[128,512]{1,0:T(8,128)(2,1)S(1)}, bf16[128,512]{1,0:T(8,128)(2,1)S(1)}, u32[]{:S(2)}, u32[]{:S(2)}) collective-permute-start(bf16[128,512]{1,0:T(8,128)(2,1)S(1)} %copy-done.3), channel_id=1, source_target_pairs={{0,8},{8,16},{16,24},{24,0},{1,9},{9,17},{17,25},{25,1},{2,10},{10... | collective-permute-start | bytes 393224 | tf_op jit(solution)/shard_map/ppermute | solution.py:253
  50.1 2.4 %copy-start.4 = (bf16[128,512]{1,0:T(8,128)(2,1)}, bf16[128,512]{1,0:T(8,128)(2,1)S(1)}, u32[]{:S(2)}) copy-start(bf16[128,512]{1,0:T(8,128)(2,1)S(1)} %collective-permute-done.q1_ref) | copy-start | bytes 393220
  50.1 2.4 %copy-start.5 = (bf16[128,512]{1,0:T(8,128)(2,1)}, bf16[128,512]{1,0:T(8,128)(2,1)S(1)}, u32[]{:S(2)}) copy-start(bf16[128,512]{1,0:T(8,128)(2,1)S(1)} %collective-permute-done.1.q2_ref) | copy-start | bytes 393220
  52.5 0.7 copy-start.6
  52.5 1.0 copy-start
  76.5 11.1 %collective-permute-start.3 = (bf16[128,512]{1,0:T(8,128)(2,1)}, bf16[128,512]{1,0:T(8,128)(2,1)S(1)}, u32[]{:S(2)}, u32[]{:S(2)}) collective-permute-start(bf16[128,512]{1,0:T(8,128)(2,1)} %combine.1.own_ref), channel_id=1, source_target_pairs={{0,1},{1,0},{2,3},{3,2},{4,5},{5,4},{6,7},{7,6},{8,9},{9,8},{10,11... | collective-permute-start | bytes 393224 | tf_op jit(solution)/shard_map/ppermute | solution.py:261
  87.5 0.7 copy-start.2
  88.2 25.0 %copy-start.1 = (bf16[128,512]{1,0:T(8,128)(2,1)S(1)}, bf16[128,512]{1,0:T(8,128)(2,1)}, u32[]{:S(2)}) copy-start(bf16[128,512]{1,0:T(8,128)(2,1)} %param.11) | copy-start | bytes 393220
  88.2 30.4 %copy-start.7 = (bf16[512]{0:T(512)(128)(2,1)S(1)}, bf16[512]{0:T(512)(128)(2,1)}, u32[]{:S(2)}) copy-start(bf16[512]{0:T(512)(128)(2,1)} %param.12) | copy-start | bytes 3076
  113.9 9.5 %all-to-all-start.4 = ((f32[8,1,128]{2,1,0:T(1,128)}), f32[8,1,128]{2,1,0:T(1,128)S(1)}, u32[]{:S(2)}, u32[]{:S(2)}) async-start(f32[8,1,128]{2,1,0:T(1,128)} %broadcast_in_dim.14), calls=%async_computation.4 | async-start | bytes 8192 | tf_op jit(solution)/shard_map/all_to_all | solution.py:25

commit v3 on v2

--- a/solution.py
+++ b/solution.py
@@ -25,6 +25,10 @@
     return lax.all_to_all(stacked, axis, split_axis=0, concat_axis=0, tiled=True)
 
 
+def in_vmem(array):
+    return pltpu.with_memory_space_constraint(array, pltpu.VMEM)
+
+
 def plan_kernel(dev_ref, span_ref, o_ref, flag_ref):
     dev = dev_ref[0]
     x = dev & 3
@@ -71,6 +75,7 @@
         in_specs=[smem, smem],
         out_specs=smem,
         scratch_shapes=[pltpu.SMEM((128,), jnp.int32)],
+        compiler_params=pltpu.CompilerParams(vmem_limit_bytes=1 * 2**20),
         name="plan",
     )(dev, span_order)
 
@@ -165,7 +170,7 @@
     smem = pl.BlockSpec(memory_space=pltpu.SMEM)
     return pl.pallas_call(
         attention_kernel,
-        out_shape=jax.ShapeDtypeStruct((peers, local + STAT_ROWS, width), jnp.bfloat16),
+        out_shape=pltpu.VMEM((peers, local + STAT_ROWS, width), jnp.bfloat16),
         in_specs=[smem] + [vmem] * (peers + 1),
         out_specs=vmem,
         scratch_shapes=[
@@ -177,8 +182,9 @@
             pltpu.VMEM((peers, 3, rows, HEAD_SIZE), jnp.float32),
             pltpu.VMEM((peers, 3, rows, HEAD_SIZE), jnp.float32),
         ],
+        compiler_params=pltpu.CompilerParams(vmem_limit_bytes=24 * 2**20),
         name="attend",
-    )(table, *queries, kv)
+    )(table, *[in_vmem(a) for a in queries], in_vmem(kv))
 
 
 def combine_kernel(p_ref, o_ref):
@@ -207,39 +213,68 @@
     vmem = pl.BlockSpec(memory_space=pltpu.VMEM)
     return pl.pallas_call(
         combine_kernel,
-        out_shape=jax.ShapeDtypeStruct((2 * SPAN, width), jnp.bfloat16),
+        out_shape=pltpu.VMEM((2 * SPAN, width), jnp.bfloat16),
         in_specs=[vmem],
         out_specs=vmem,
+        compiler_params=pltpu.CompilerParams(vmem_limit_bytes=4 * 2**20),
         name="combine",
-    )(parts)
-
-
-def project_kernel(core_ref, own_ref, other_ref, w_ref, w2_ref, o_ref):
-    out = jnp.dot(own_ref[...], w_ref[...], preferred_element_type=jnp.float32)
-    out = out + jnp.dot(other_ref[...], w2_ref[...], preferred_element_type=jnp.float32)
-    o_ref[0] = out.astype(jnp.bfloat16)
-
-
-def project(core, own, other, weight, weight_other):
-    rows, width = own.shape
+    )(in_vmem(parts))
+
+
+def split_kernel(core_ref, w_ref, keep_ref, send_ref, sem):
+    core = core_ref[0]
     block = 512
-    chips = weight.shape[1] // block // 2
+    moves = []
+    for z in range(keep_ref.shape[1] // block):
+        for ref, which in ((keep_ref, core), (send_ref, 1 - core)):
+            at = pl.multiple_of((2 * z + which) * block, block)
+            src = w_ref.at[:, pl.ds(at, block)]
+            moves.append(pltpu.make_async_copy(src, ref.at[:, z * block : (z + 1) * block], sem.at[len(moves)]))
+    for move in moves:
+        move.start()
+    for move in moves:
+        move.wait()
+
+
+def split(core, weight):
+    rows, width = weight.shape
+    vmem = pl.BlockSpec(memory_space=pltpu.VMEM)
+    smem = pl.BlockSpec(memory_space=pltpu.SMEM)
+    half = pltpu.VMEM((rows, width // 2), jnp.bfloat16)
+    return pl.pallas_call(
+        split_kernel,
+        in_specs=[smem, pl.BlockSpec(memory_space=pltpu.HBM)],
+        out_specs=(vmem, vmem),
+        out_shape=(half, half),
+        scratch_shapes=[pltpu.SemaphoreType.DMA((8,))],
+        compiler_params=pltpu.CompilerParams(vmem_limit_bytes=2 * 2**20),
+        name="split",
+    )(core, pltpu.with_memory_space_constraint(weight, pltpu.HBM))
+
+
+def project_kernel(own_ref, other_ref, w_ref, w2_ref, o_ref):
+    chips, _, block = o_ref.shape
+    own = own_ref[...]
+    other = other_ref[...]
+    for z in range(chips):
+        cols = slice(z * block, (z + 1) * block)
+        out = jnp.dot(own, w_ref[:, cols], preferred_element_type=jnp.float32)
+        out = out + jnp.dot(other, w2_ref[:, cols], preferred_element_type=jnp.float32)
+        o_ref[z] = out.astype(jnp.bfloat16)
+
+
+def project(own, other, weight, weight_other):
+    rows = own.shape[0]
+    block = 512
+    vmem = pl.BlockSpec(memory_space=pltpu.VMEM)
     return pl.pallas_call(
         project_kernel,
-        grid_spec=pltpu.PrefetchScalarGridSpec(
-            num_scalar_prefetch=1,
-            grid=(chips,),
-            in_specs=[
-                pl.BlockSpec((rows, width), lambda z, c: (0, 0)),
-                pl.BlockSpec((rows, width), lambda z, c: (0, 0)),
-                pl.BlockSpec((width, block), lambda z, c: (0, 2 * z + c[0])),
-                pl.BlockSpec((width, block), lambda z, c: (0, 2 * z + c[0])),
-            ],
-            out_specs=pl.BlockSpec((1, rows, block), lambda z, c: (z, 0, 0)),
-        ),
-        out_shape=jax.ShapeDtypeStruct((chips, rows, block), jnp.bfloat16),
+        in_specs=[vmem] * 4,
+        out_specs=vmem,
+        out_shape=pltpu.VMEM((weight.shape[1] // block, rows, block), jnp.bfloat16),
+        compiler_params=pltpu.CompilerParams(vmem_limit_bytes=4 * 2**20),
         name="project",
-    )(core, own, other, weight, weight_other)
+    )(*[in_vmem(a) for a in (own, other, weight, weight_other)])
 
 
 def per_device(queries, keys, values, out_weight, residual, norm_gain, span_order):
@@ -251,15 +286,16 @@
     kv = copies(jnp.concatenate((keys, values), axis=1), "zh")
     rows = kv.shape[0] * kv.shape[1]
     qs = [queries] + [lax.ppermute(queries, "x", [(i, (i - d) % 4) for i in range(4)]) for d in (1, 2, 3)]
-    weight_other = lax.ppermute(out_weight, "c", swap)
     kv = copies(kv.reshape(rows, kv.shape[2]), "y")
+    weight, weight_send = split(core.reshape(1), out_weight)
+    weight_other = lax.ppermute(weight_send, "c", swap)
     table = plan(((y * 4 + zh) * 4 + x).reshape(1), span_order)
     kv = kv.reshape(kv.shape[0] * rows, kv.shape[2])
     parts = attend(table, qs, kv)
     parts = lax.all_to_all(parts, "x", 0, 0, tiled=True)
     attended = combine(parts)
     attended_other = lax.ppermute(attended, "c", swap)
-    partial_sums = project(core.reshape(1), attended, attended_other, out_weight, weight_other)
+    partial_sums = project(attended, attended_other, weight, weight_other)
     share = lax.all_to_all(partial_sums, "zl", 0, 0, tiled=True)
     projected = jnp.sum(share.astype(jnp.float32), axis=0)
     hidden = (residual.astype(jnp.float32) + projected).astype(jnp.bfloat16)

time: 125 us -> 113 us (0.904)
  blocking collectives: 55.5 us -> 28.3 us
  starting transfers between devices: 36.8 us -> 47.5 us
  waiting for transfers between devices: 8.42 us -> 15.5 us
  Pallas kernels: 18.2 us -> 16.3 us
    all_to_all x1 -> x0, blocking collectives: 23.6 us -> none  [copies(): lax.all_to_all(stacked, axis, split_axis=0, concat_axis=0, tiled=True)]
    all_to_all x2 -> x3, starting transfers between devices: 8.79 us -> 24.4 us  [copies(): lax.all_to_all(stacked, axis, split_axis=0, concat_axis=0, tiled=True)]
    all_to_all x2 -> x3, waiting for transfers between devices: 4.84 us -> 12 us  [copies(): lax.all_to_all(stacked, axis, split_axis=0, concat_axis=0, tiled=True)]
    ppermute x1, starting transfers between devices: 8.87 us -> 3 us  [per_device(): weight_other = lax.ppermute(weight_send, 'c', swap)]
    all_to_all x1, blocking collectives: 11.5 us -> 9.66 us  [per_device(): parts = lax.all_to_all(parts, 'x', 0, 0, tiled=True)]
    pallas_call x3 -> x4, Pallas kernels: 16 us -> 14.2 us  [the longest x1 7.75 us: attend(): pl.pallas_call(attention_kernel, out_shape=pltpu.VMEM((peers, local + STA...]
    all_to_all x1, blocking collectives: 20.4 us -> 18.6 us  [per_device(): share = lax.all_to_all(partial_sums, 'zl', 0, 0, tiled=True)]
    unnamed x16 -> x8, local copies, waits for them, and re-layouts: 1.66 us -> 0.02 us
  transfers between devices with their start and end apart: 7 -> 8, of which waited for: 3 -> 5; matrix products, arithmetic and copies ran while one was open for 1% -> 1% of each run, Pallas kernels for 11% -> 13%
where the time goes in v3:
time: 113 us; the launch traced here: 112 us
  starting transfers between devices  47.5 us (42%)
  blocking collectives  28.3 us (25%)
  Pallas kernels  16.3 us (14%)
  waiting for transfers between devices  15.5 us (14%)
  local copies, waits for them, and re-layouts  2.38 us (2%)
  other arithmetic  1.75 us (2%)
    all_to_all x3, starting transfers between devices, copies(): lax.all_to_all(stacked, axis, split_axis=0, concat_axis=0, tiled=True)  24.4 us
    all_to_all x1, blocking collectives, per_device(): share = lax.all_to_all(partial_sums, 'zl', 0, 0, tiled=True)  18.6 us
    all_to_all x3, waiting for transfers between devices, copies(): lax.all_to_all(stacked, axis, split_axis=0, concat_axis=0, tiled=True)  12 us
    ppermute x1, starting transfers between devices, per_device(): attended_other = lax.ppermute(attended, 'c', swap)  10.8 us
    all_to_all x1, blocking collectives, per_device(): parts = lax.all_to_all(parts, 'x', 0, 0, tiled=True)  9.66 us
    ppermute x3, starting transfers between devices, per_device(): lax.ppermute(queries, 'x', [(i, (i - d) % 4) for i in range(4)])  9.32 us
    pallas_call x1, Pallas kernels, attend(): pl.pallas_call(attention_kernel, out_shape=pltpu.VMEM((peers, local + STA...  7.75 us
    pallas_call x1, Pallas kernels, split(): pl.pallas_call(split_kernel, in_specs=[smem, pl.BlockSpec(memory_space=pl...  3.59 us
  transfers between devices with their start and end apart: 8, of which 5 were waited for; matrix products, arithmetic and copies ran while one was open for 1% of the time, Pallas kernels for 13%

profile of v3, /device:TPU:1, one launch (start us, length us, event | category | flops | bytes accessed | tf_op | source)
XLA Modules:
  0.0 111.9 jit_solution(6879031231568857691)
XLA Ops:
  0.0 0.8 pad_maximum_fusion
  0.8 0.7 broadcast_in_dim.12
  1.5 15.6 %all-to-all-start = ((bf16[4,128,256]{2,1,0:T(8,128)(2,1)}), bf16[4,128,256]{2,1,0:T(8,128)(2,1)S(1)}, u32[]{:S(2)}, u32[]{:S(2)}) async-start(bf16[4,128,256]{2,1,0:T(8,128)(2,1)} %broadcast_in_dim.12), calls=%async_computation | async-start | bytes 524288 | tf_op jit(solution)/shard_map/all_to_all | solution.py:25
  17.1 3.6 %split.1 = (bf16[512,2048]{1,0:T(8,128)(2,1)S(1)}, bf16[512,2048]{1,0:T(8,128)(2,1)}) custom-call(s32[1]{0:T(128)} %bitcast.3.core_ref, bf16[512,4096]{1,0:T(8,128)(2,1)} %w_ref.1), custom_call_target="tpu_custom_call" | custom-call | tf_op jit(solution)/shard_map/split/pallas_call | solution.py:244
  20.7 0.0 copy-start
  20.7 0.0 copy-start.1
  20.7 3.0 %collective-permute-start.4 = (bf16[512,2048]{1,0:T(8,128)(2,1)}, bf16[512,2048]{1,0:T(8,128)(2,1)}, u32[]{:S(2)}, u32[]{:S(2)}) collective-permute-start(bf16[512,2048]{1,0:T(8,128)(2,1)} %get-tuple-element.8), channel_id=1, source_target_pairs={{0,1},{1,0},{2,3},{3,2},{4,5},{5,4},{6,7},{7,6},{8,9},{9,8},{10,11... | collective-permute-start | bytes 6291464 | tf_op jit(solution)/shard_map/ppermute | solution.py:291
  23.8 7.2 %all-to-all-done = bf16[4,128,256]{2,1,0:T(8,128)(2,1)S(1)} async-done(((bf16[4,128,256]{2,1,0:T(8,128)(2,1)}), bf16[4,128,256]{2,1,0:T(8,128)(2,1)S(1)}, u32[]{:S(2)}, u32[]{:S(2)}) %all-to-all-start) | async-done | bytes 262176 | tf_op jit(solution)/shard_map/all_to_all | solution.py:25
  30.9 1.0 broadcast_in_dim.13
  32.0 4.2 %all-to-all-start.1 = ((bf16[4,512,256]{2,1,0:T(8,128)(2,1)}), bf16[4,512,256]{2,1,0:T(8,128)(2,1)S(1)}, u32[]{:S(2)}, u32[]{:S(2)}) async-start(bf16[4,512,256]{2,1,0:T(8,128)(2,1)} %broadcast_in_dim.13), calls=%async_computation.1 | async-start | bytes 2097152 | tf_op jit(solution)/shard_map/all_to_all | solution.py:25
  36.1 0.0 copy-done
  36.2 4.4 %collective-permute-start = (bf16[128,512]{1,0:T(8,128)(2,1)S(1)}, bf16[128,512]{1,0:T(8,128)(2,1)S(1)}, u32[]{:S(2)}, u32[]{:S(2)}) collective-permute-start(bf16[128,512]{1,0:T(8,128)(2,1)S(1)} %copy-done), channel_id=1, source_target_pairs={{0,24},{8,0},{16,8},{24,16},{1,25},{9,1},{17,9},{25,17},{2,26},{10... | collective-permute-start | bytes 393224 | tf_op jit(solution)/shard_map/ppermute | solution.py:288
  40.5 2.4 %collective-permute-start.1 = (bf16[128,512]{1,0:T(8,128)(2,1)S(1)}, bf16[128,512]{1,0:T(8,128)(2,1)S(1)}, u32[]{:S(2)}, u32[]{:S(2)}) collective-permute-start(bf16[128,512]{1,0:T(8,128)(2,1)S(1)} %copy-done), channel_id=1, source_target_pairs={{0,16},{8,24},{16,0},{24,8},{1,17},{9,25},{17,1},{25,9},{2,18},{10... | collective-permute-start | bytes 393224 | tf_op jit(solution)/shard_map/ppermute | solution.py:288
  43.0 2.5 %collective-permute-start.2 = (bf16[128,512]{1,0:T(8,128)(2,1)S(1)}, bf16[128,512]{1,0:T(8,128)(2,1)}, u32[]{:S(2)}, u32[]{:S(2)}) collective-permute-start(bf16[128,512]{1,0:T(8,128)(2,1)S(1)} %copy-done), channel_id=1, source_target_pairs={{0,8},{8,16},{16,24},{24,0},{1,9},{9,17},{17,25},{25,1},{2,10},{10... | collective-permute-start | bytes 393224 | tf_op jit(solution)/shard_map/ppermute | solution.py:288
  45.5 0.0 copy-done.1
  45.5 2.1 %plan.1.tab_ref = s32[256]{0:T(256)S(1)} custom-call(s32[1]{0:T(128)} %bitcast.dev_ref, s32[128]{0:T(128)S(1)} %copy-done.1), custom_call_target="tpu_custom_call" | custom-call | tf_op jit(solution)/shard_map/plan/pallas_call | solution.py:72
  47.7 0.0 collective-permute-done.q1_ref
  47.7 0.1 collective-permute-done.1.q2_ref
  47.8 2.4 %collective-permute-done.2.q3_ref = bf16[128,512]{1,0:T(8,128)(2,1)} collective-permute-done((bf16[128,512]{1,0:T(8,128)(2,1)S(1)}, bf16[128,512]{1,0:T(8,128)(2,1)}, u32[]{:S(2)}, u32[]{:S(2)}) %collective-permute-start.2) | collective-permute-done | bytes 131104 | tf_op jit(solution)/shard_map/ppermute | solution.py:288
  50.2 0.0 all-to-all-done.1
  50.2 7.8 %attend.1 = bf16[4,144,512]{2,1,0:T(8,128)(2,1)S(1)} custom-call(s32[256]{0:T(256)S(1)} %plan.1.tab_ref, bf16[128,512]{1,0:T(8,128)(2,1)S(1)} %copy-done, bf16[128,512]{1,0:T(8,128)(2,1)S(1)} %collective-permute-done.q1_ref, bf16[128,512]{1,0:T(8,128)(2,1)S(1)} %collective-permute-done.1.q2_ref, bf16[128,512]{1,0:T(8,128)(2,1)} %collective-permute-done.2.q3_ref, ...), custom_call_target="tpu_custom_call" | custom-call | tf_op jit(solution)/shard_map/attend/pallas_call | solution.py:171
  57.9 9.7 %all_to_all.25.p_ref = bf16[4,144,512]{2,1,0:T(8,128)(2,1)S(1)} all-to-all(bf16[4,144,512]{2,1,0:T(8,128)(2,1)S(1)} %attend.1), channel_id=1, replica_groups=mesh['y'=4,'zh'=4,'x'=4,'zl'=4,'c'=2] {'x'}, dimensions={0} | all-to-all | bytes 1179648 | tf_op jit(solution)/shard_map/all_to_all | solution.py:295
  67.6 0.5 combine.1.own_ref
  68.1 10.8 %collective-permute-start.3 = (bf16[128,512]{1,0:T(8,128)(2,1)S(1)}, bf16[128,512]{1,0:T(8,128)(2,1)S(1)}, u32[]{:S(2)}, u32[]{:S(2)}) collective-permute-start(bf16[128,512]{1,0:T(8,128)(2,1)S(1)} %combine.1.own_ref), channel_id=1, source_target_pairs={{0,1},{1,0},{2,3},{3,2},{4,5},{5,4},{6,7},{7,6},{8,9},{9,8},{10,11... | collective-permute-start | bytes 393224 | tf_op jit(solution)/shard_map/ppermute | solution.py:297
  78.9 0.0 collective-permute-done.4.w2_ref
  78.9 1.0 collective-permute-done.3.other_ref
  79.9 0.0 copy-start.2
  79.9 2.3 %project.1 = bf16[4,128,512]{2,1,0:T(8,128)(2,1)S(1)} custom-call(bf16[128,512]{1,0:T(8,128)(2,1)S(1)} %combine.1.own_ref, bf16[128,512]{1,0:T(8,128)(2,1)S(1)} %collective-permute-done.3.other_ref, bf16[512,2048]{1,0:T(8,128)(2,1)S(1)} %get-tuple-element.7.w_ref, bf16[512,2048]{1,0:T(8,128)(2,1)} %collective-permute-done.4.w2_ref), custom_call_target="tpu_custom_call" | custom-call | tf_op jit(solution)/shard_map/project/pallas_call | solution.py:270
  82.2 0.0 copy-start.3
  82.2 18.6 %all_to_all.26 = bf16[4,128,512]{2,1,0:T(8,128)(2,1)S(1)} all-to-all(bf16[4,128,512]{2,1,0:T(8,128)(2,1)S(1)} %project.1), channel_id=1, replica_groups=mesh['y'=4,'zh'=4,'x'=4,'zl'=4,'c'=2] {'zl'}, dimensions={0} | all-to-all | bytes 1048576 | tf_op jit(solution)/shard_map/all_to_all | solution.py:299
  100.9 0.1 convert_reduce_fusion
  100.9 0.0 copy-done.2
  101.0 0.1 fusion
  101.1 0.6 broadcast_in_dim.14
  101.7 4.6 %all-to-all-start.4 = ((f32[8,1,128]{2,1,0:T(1,128)}), f32[8,1,128]{2,1,0:T(1,128)S(1)}, u32[]{:S(2)}, u32[]{:S(2)}) async-start(f32[8,1,128]{2,1,0:T(1,128)} %broadcast_in_dim.14), calls=%async_computation.4 | async-start | bytes 8192 | tf_op jit(solution)/shard_map/all_to_all | solution.py:25
  106.3 0.0 copy-done.3
  106.3 4.8 %all-to-all-done.4 = f32[8,1,128]{2,1,0:T(1,128)S(1)} async-done(((f32[8,1,128]{2,1,0:T(1,128)}), f32[8,1,128]{2,1,0:T(1,128)S(1)}, u32[]{:S(2)}, u32[]{:S(2)}) %all-to-all-start.4) | async-done | bytes 4128 | tf_op jit(solution)/shard_map/all_to_all | solution.py:25
  111.2 0.8 fusion.2
  (3 shorter events, 0.0 us)
Async XLA Ops:
  1.5 29.4 %all-to-all-start = ((bf16[4,128,256]{2,1,0:T(8,128)(2,1)}), bf16[4,128,256]{2,1,0:T(8,128)(2,1)S(1)}, u32[]{:S(2)}, u32[]{:S(2)}) async-start(bf16[4,128,256]{2,1,0:T(8,128)(2,1)} %broadcast_in_dim.12), calls=%async_computation | async-start | bytes 524288 | tf_op jit(solution)/shard_map/all_to_all | solution.py:25
  20.7 15.4 %copy-start = (bf16[128,512]{1,0:T(8,128)(2,1)S(1)}, bf16[128,512]{1,0:T(8,128)(2,1)}, u32[]{:S(2)}) copy-start(bf16[128,512]{1,0:T(8,128)(2,1)} %q0_ref.1) | copy-start | bytes 393220
  20.7 24.8 %copy-start.1 = (s32[128]{0:T(128)S(1)}, s32[128]{0:T(128)}, u32[]{:S(2)}) copy-start(s32[128]{0:T(128)} %span_ref.1) | copy-start | bytes 1540
  20.7 58.1 %collective-permute-start.4 = (bf16[512,2048]{1,0:T(8,128)(2,1)}, bf16[512,2048]{1,0:T(8,128)(2,1)}, u32[]{:S(2)}, u32[]{:S(2)}) collective-permute-start(bf16[512,2048]{1,0:T(8,128)(2,1)} %get-tuple-element.8), channel_id=1, source_target_pairs={{0,1},{1,0},{2,3},{3,2},{4,5},{5,4},{6,7},{7,6},{8,9},{9,8},{10,11... | collective-permute-start | bytes 6291464 | tf_op jit(solution)/shard_map/ppermute | solution.py:291
  32.0 18.2 %all-to-all-start.1 = ((bf16[4,512,256]{2,1,0:T(8,128)(2,1)}), bf16[4,512,256]{2,1,0:T(8,128)(2,1)S(1)}, u32[]{:S(2)}, u32[]{:S(2)}) async-start(bf16[4,512,256]{2,1,0:T(8,128)(2,1)} %broadcast_in_dim.13), calls=%async_computation.1 | async-start | bytes 2097152 | tf_op jit(solution)/shard_map/all_to_all | solution.py:25
  36.2 11.5 %collective-permute-start = (bf16[128,512]{1,0:T(8,128)(2,1)S(1)}, bf16[128,512]{1,0:T(8,128)(2,1)S(1)}, u32[]{:S(2)}, u32[]{:S(2)}) collective-permute-start(bf16[128,512]{1,0:T(8,128)(2,1)S(1)} %copy-done), channel_id=1, source_target_pairs={{0,24},{8,0},{16,8},{24,16},{1,25},{9,1},{17,9},{25,17},{2,26},{10... | collective-permute-start | bytes 393224 | tf_op jit(solution)/shard_map/ppermute | solution.py:288
  40.5 7.2 %collective-permute-start.1 = (bf16[128,512]{1,0:T(8,128)(2,1)S(1)}, bf16[128,512]{1,0:T(8,128)(2,1)S(1)}, u32[]{:S(2)}, u32[]{:S(2)}) collective-permute-start(bf16[128,512]{1,0:T(8,128)(2,1)S(1)} %copy-done), channel_id=1, source_target_pairs={{0,16},{8,24},{16,0},{24,8},{1,17},{9,25},{17,1},{25,9},{2,18},{10... | collective-permute-start | bytes 393224 | tf_op jit(solution)/shard_map/ppermute | solution.py:288
  43.0 7.2 %collective-permute-start.2 = (bf16[128,512]{1,0:T(8,128)(2,1)S(1)}, bf16[128,512]{1,0:T(8,128)(2,1)}, u32[]{:S(2)}, u32[]{:S(2)}) collective-permute-start(bf16[128,512]{1,0:T(8,128)(2,1)S(1)} %copy-done), channel_id=1, source_target_pairs={{0,8},{8,16},{16,24},{24,0},{1,9},{9,17},{17,25},{25,1},{2,10},{10... | collective-permute-start | bytes 393224 | tf_op jit(solution)/shard_map/ppermute | solution.py:288
  68.1 11.7 %collective-permute-start.3 = (bf16[128,512]{1,0:T(8,128)(2,1)S(1)}, bf16[128,512]{1,0:T(8,128)(2,1)S(1)}, u32[]{:S(2)}, u32[]{:S(2)}) collective-permute-start(bf16[128,512]{1,0:T(8,128)(2,1)S(1)} %combine.1.own_ref), channel_id=1, source_target_pairs={{0,1},{1,0},{2,3},{3,2},{4,5},{5,4},{6,7},{7,6},{8,9},{9,8},{10,11... | collective-permute-start | bytes 393224 | tf_op jit(solution)/shard_map/ppermute | solution.py:297
  79.9 21.1 %copy-start.2 = (bf16[128,512]{1,0:T(8,128)(2,1)S(1)}, bf16[128,512]{1,0:T(8,128)(2,1)}, u32[]{:S(2)}) copy-start(bf16[128,512]{1,0:T(8,128)(2,1)} %param.11) | copy-start | bytes 393220
  82.2 24.1 %copy-start.3 = (bf16[512]{0:T(512)(128)(2,1)S(1)}, bf16[512]{0:T(512)(128)(2,1)}, u32[]{:S(2)}) copy-start(bf16[512]{0:T(512)(128)(2,1)} %param.12) | copy-start | bytes 3076
  101.7 9.5 %all-to-all-start.4 = ((f32[8,1,128]{2,1,0:T(1,128)}), f32[8,1,128]{2,1,0:T(1,128)S(1)}, u32[]{:S(2)}, u32[]{:S(2)}) async-start(f32[8,1,128]{2,1,0:T(1,128)} %broadcast_in_dim.14), calls=%async_computation.4 | async-start | bytes 8192 | tf_op jit(solution)/shard_map/all_to_all | solution.py:25

commit v4 on v3

--- a/solution.py
+++ b/solution.py
@@ -20,13 +20,32 @@
 STAT_ROWS = 16
 
 
-def copies(shard, axis):
-    stacked = jnp.broadcast_to(shard, (lax.axis_size(axis), *shard.shape))
-    return lax.all_to_all(stacked, axis, split_axis=0, concat_axis=0, tiled=True)
-
-
 def in_vmem(array):
     return pltpu.with_memory_space_constraint(array, pltpu.VMEM)
+
+
+def spread_kernel(*refs):
+    o_ref = refs[-1]
+    at = 0
+    for ref in refs[:-1]:
+        part = ref[...]
+        for i in range(o_ref.shape[0]):
+            o_ref[i, :, at : at + part.shape[1]] = part
+        at += part.shape[1]
+
+
+def spread(arrays, copies):
+    rows = arrays[0].shape[0]
+    width = sum(a.shape[1] for a in arrays)
+    vmem = pl.BlockSpec(memory_space=pltpu.VMEM)
+    return pl.pallas_call(
+        spread_kernel,
+        in_specs=[vmem] * len(arrays),
+        out_specs=vmem,
+        out_shape=pltpu.VMEM((copies, rows, width), arrays[0].dtype),
+        compiler_params=pltpu.CompilerParams(vmem_limit_bytes=2 * 2**20),
+        name="spread",
+    )(*arrays)
 
 
 def plan_kernel(dev_ref, span_ref, o_ref, flag_ref):
@@ -114,33 +133,37 @@
             q_half = half if b < 2 else jnp.minimum(half, 1)
             q = q_ref[pl.ds(pl.multiple_of((peer * 2 + q_half) * rows, rows), rows), :]
             k = k_ref[pl.ds(pl.multiple_of(kb * block, block), block), :]
-            s = lax.dot_general(q, k, (((1,), (1,)), ((), ())), preferred_element_type=jnp.float32)
             if b < 2:
                 qspan = tab_ref[2 * peer + half]
                 limits = [(qspan - tab_ref[64 + 4 * kb + j]) * SPAN for j in range(4)]
                 limit = jnp.full((1, block), limits[0], jnp.int32)
                 for j in range(1, 4):
                     limit = jnp.where(lane_row >= j, limits[j], limit)
-                s = jnp.where(diff <= limit, s, NEG)
-            s_ref[b] = s
-            top = jnp.maximum(s[:, :lanes], s[:, lanes:])
-            mx_ref[half] = top if b < 2 else jnp.maximum(mx_ref[half], top)
+            for r in range(0, rows, 128):
+                part = slice(r, r + 128)
+                s = lax.dot_general(q[part], k, (((1,), (1,)), ((), ())), preferred_element_type=jnp.float32)
+                if b < 2:
+                    s = jnp.where(diff[part] <= limit, s, NEG)
+                s_ref[b, part] = s
+                top = jnp.maximum(s[:, :lanes], s[:, lanes:])
+                mx_ref[half, part] = top if b < 2 else jnp.maximum(mx_ref[half, part], top)
         for half in range(2):
             mx_ref[half] = jnp.broadcast_to(jnp.max(mx_ref[half], axis=1, keepdims=True), (rows, lanes))
         for b, (half, kb) in enumerate(work):
-            m = mx_ref[half]
-            s = s_ref[b]
-            w0 = jnp.exp2((s[:, :lanes] - m) * (SCALE * LOG2E))
-            w1 = jnp.exp2((s[:, lanes:] - m) * (SCALE * LOG2E))
             v = v_ref[pl.ds(pl.multiple_of(kb * block, block), block), :]
-            w = jnp.concatenate([w0.astype(jnp.bfloat16), w1.astype(jnp.bfloat16)], axis=1)
-            out = jnp.dot(w, v, preferred_element_type=jnp.float32)
-            if b < 2:
-                l_ref[half] = w0 + w1
-                acc_ref[half] = out
-            else:
-                l_ref[half] = l_ref[half] + (w0 + w1)
-                acc_ref[half] = acc_ref[half] + out
+            for r in range(0, rows, 128):
+                part = slice(r, r + 128)
+                m = mx_ref[half, part]
+                w0 = jnp.exp2((s_ref[b, part, :lanes] - m) * (SCALE * LOG2E))
+                w1 = jnp.exp2((s_ref[b, part, lanes:] - m) * (SCALE * LOG2E))
+                w = jnp.concatenate([w0.astype(jnp.bfloat16), w1.astype(jnp.bfloat16)], axis=1)
+                out = jnp.dot(w, v, preferred_element_type=jnp.float32)
+                if b < 2:
+                    l_ref[half, part] = w0 + w1
+                    acc_ref[half, part] = out
+                else:
+                    l_ref[half, part] = l_ref[half, part] + (w0 + w1)
+                    acc_ref[half, part] = acc_ref[half, part] + out
         dest = tab_ref[16 + peer]
         which = lax.broadcasted_iota(jnp.int32, (rows, lanes), 1)
         for half in range(2):
@@ -221,60 +244,85 @@
     )(in_vmem(parts))
 
 
-def split_kernel(core_ref, w_ref, keep_ref, send_ref, sem):
-    core = core_ref[0]
-    block = 512
+def columns_kernel(blocks, at_ref, w_ref, w2_ref, o_ref, o2_ref, sem):
+    core = at_ref[0] & 1
+    place = at_ref[0] >> 1
+    width = o_ref.shape[1] // len(blocks)
     moves = []
-    for z in range(keep_ref.shape[1] // block):
-        for ref, which in ((keep_ref, core), (send_ref, 1 - core)):
-            at = pl.multiple_of((2 * z + which) * block, block)
-            src = w_ref.at[:, pl.ds(at, block)]
-            moves.append(pltpu.make_async_copy(src, ref.at[:, z * block : (z + 1) * block], sem.at[len(moves)]))
+    for i, d in enumerate(blocks):
+        at = pl.multiple_of((2 * (place ^ d) + core) * width, width)
+        for src, dst in ((w_ref, o_ref), (w2_ref, o2_ref)):
+            dst = dst.at[:, i * width : (i + 1) * width]
+            moves.append(pltpu.make_async_copy(src.at[:, pl.ds(at, width)], dst, sem.at[len(moves)]))
     for move in moves:
         move.start()
     for move in moves:
         move.wait()
 
 
-def split(core, weight):
-    rows, width = weight.shape
-    vmem = pl.BlockSpec(memory_space=pltpu.VMEM)
-    smem = pl.BlockSpec(memory_space=pltpu.SMEM)
-    half = pltpu.VMEM((rows, width // 2), jnp.bfloat16)
-    return pl.pallas_call(
-        split_kernel,
-        in_specs=[smem, pl.BlockSpec(memory_space=pltpu.HBM)],
+def columns(blocks, place, weight, weight_other):
+    rows = weight.shape[0]
+    vmem = pl.BlockSpec(memory_space=pltpu.VMEM)
+    hbm = pl.BlockSpec(memory_space=pltpu.HBM)
+    return pl.pallas_call(
+        functools.partial(columns_kernel, blocks),
+        in_specs=[pl.BlockSpec(memory_space=pltpu.SMEM), hbm, hbm],
         out_specs=(vmem, vmem),
-        out_shape=(half, half),
-        scratch_shapes=[pltpu.SemaphoreType.DMA((8,))],
+        out_shape=(pltpu.VMEM((rows, 512 * len(blocks)), jnp.bfloat16),) * 2,
+        scratch_shapes=[pltpu.SemaphoreType.DMA((2 * len(blocks),))],
         compiler_params=pltpu.CompilerParams(vmem_limit_bytes=2 * 2**20),
-        name="split",
-    )(core, pltpu.with_memory_space_constraint(weight, pltpu.HBM))
-
-
-def project_kernel(own_ref, other_ref, w_ref, w2_ref, o_ref):
-    chips, _, block = o_ref.shape
+        name="columns",
+    )(place, *[pltpu.with_memory_space_constraint(w, pltpu.HBM) for w in (weight, weight_other)])
+
+
+def project_kernel(own_ref, other_ref, w_ref, w2_ref, *o_refs):
+    width = o_refs[0].shape[1]
     own = own_ref[...]
     other = other_ref[...]
-    for z in range(chips):
-        cols = slice(z * block, (z + 1) * block)
+    for i, o_ref in enumerate(o_refs):
+        cols = slice(i * width, (i + 1) * width)
         out = jnp.dot(own, w_ref[:, cols], preferred_element_type=jnp.float32)
         out = out + jnp.dot(other, w2_ref[:, cols], preferred_element_type=jnp.float32)
-        o_ref[z] = out.astype(jnp.bfloat16)
-
-
-def project(own, other, weight, weight_other):
+        o_ref[...] = out.astype(o_ref.dtype)
+
+
+def project(blocks, own, other, weight, weight_other):
     rows = own.shape[0]
-    block = 512
     vmem = pl.BlockSpec(memory_space=pltpu.VMEM)
     return pl.pallas_call(
         project_kernel,
         in_specs=[vmem] * 4,
-        out_specs=vmem,
-        out_shape=pltpu.VMEM((weight.shape[1] // block, rows, block), jnp.bfloat16),
+        out_specs=tuple(vmem for d in blocks),
+        out_shape=tuple(pltpu.VMEM((rows, 512), jnp.bfloat16 if d else jnp.float32) for d in blocks),
         compiler_params=pltpu.CompilerParams(vmem_limit_bytes=4 * 2**20),
         name="project",
     )(*[in_vmem(a) for a in (own, other, weight, weight_other)])
+
+
+def total_kernel(p0_ref, p1_ref, p2_ref, p3_ref, r_ref, h_ref, s_ref):
+    total = p0_ref[...]
+    for ref in (p1_ref, p2_ref, p3_ref):
+        total = total + ref[...].astype(jnp.float32)
+    hidden = (r_ref[...].astype(jnp.float32) + total).astype(jnp.bfloat16)
+    h_ref[...] = hidden
+    hidden = hidden.astype(jnp.float32)
+    squares = jnp.sum(hidden * hidden, axis=1, keepdims=True)
+    row = jnp.broadcast_to(squares, (squares.shape[0], 128)).T[:1]
+    for i in range(s_ref.shape[0]):
+        s_ref[i] = row
+
+
+def total(parts, residual):
+    rows, width = residual.shape
+    vmem = pl.BlockSpec(memory_space=pltpu.VMEM)
+    return pl.pallas_call(
+        total_kernel,
+        in_specs=[vmem] * 5,
+        out_specs=(vmem, vmem),
+        out_shape=(pltpu.VMEM((rows, width), jnp.bfloat16), pltpu.VMEM((8, 1, rows), jnp.float32)),
+        compiler_params=pltpu.CompilerParams(vmem_limit_bytes=4 * 2**20),
+        name="total",
+    )(*[in_vmem(a) for a in (*parts, residual)])
 
 
 def per_device(queries, keys, values, out_weight, residual, norm_gain, span_order):
@@ -283,24 +331,29 @@
     x = lax.axis_index("x")
     core = lax.axis_index("c")
     swap = [(0, 1), (1, 0)]
-    kv = copies(jnp.concatenate((keys, values), axis=1), "zh")
-    rows = kv.shape[0] * kv.shape[1]
-    qs = [queries] + [lax.ppermute(queries, "x", [(i, (i - d) % 4) for i in range(4)]) for d in (1, 2, 3)]
-    kv = copies(kv.reshape(rows, kv.shape[2]), "y")
-    weight, weight_send = split(core.reshape(1), out_weight)
-    weight_other = lax.ppermute(weight_send, "c", swap)
+    shift = lambda a, axis, d: lax.ppermute(a, axis, [(i, (i - d) % 4) for i in range(4)])
+    kv = jnp.concatenate((keys, values), axis=1)
+    kv = lax.all_to_all(jnp.broadcast_to(kv, (4, *kv.shape)), "zh", 0, 0, tiled=True)
+    qs = [queries] + [shift(queries, "x", d) for d in (1, 2, 3)]
+    kv = lax.all_to_all(spread((in_vmem(kv.reshape(-1, kv.shape[2])),), 4), "y", 0, 0, tiled=True)
+    weight_other = lax.ppermute(out_weight, "c", swap)
     table = plan(((y * 4 + zh) * 4 + x).reshape(1), span_order)
-    kv = kv.reshape(kv.shape[0] * rows, kv.shape[2])
-    parts = attend(table, qs, kv)
+    parts = attend(table, qs, kv.reshape(-1, kv.shape[2]))
     parts = lax.all_to_all(parts, "x", 0, 0, tiled=True)
+    place = (2 * lax.axis_index("zl") + core).reshape(1)
+    far_weights = columns((2, 3), place, out_weight, weight_other)
     attended = combine(parts)
     attended_other = lax.ppermute(attended, "c", swap)
-    partial_sums = project(attended, attended_other, weight, weight_other)
-    share = lax.all_to_all(partial_sums, "zl", 0, 0, tiled=True)
-    projected = jnp.sum(share.astype(jnp.float32), axis=0)
-    hidden = (residual.astype(jnp.float32) + projected).astype(jnp.bfloat16)
+    across = lambda a, d: lax.ppermute(a, "zl", [(i, i ^ d) for i in range(4)])
+    far2, far3 = project((2, 3), attended, attended_other, *far_weights)
+    far2 = across(far2, 2)
+    far3 = across(far3, 3)
+    near_weights = columns((0, 1), place, out_weight, weight_other)
+    own, near = project((0, 1), attended, attended_other, *near_weights)
+    near = across(near, 1)
+    hidden, squares = total((own, near, far2, far3), residual)
     hidden_f = hidden.astype(jnp.float32)
-    squares = copies(jnp.sum(hidden_f * hidden_f, axis=1)[None, :], ("zl", "c"))
+    squares = lax.all_to_all(squares, ("zl", "c"), 0, 0, tiled=True)
     squares = jnp.sum(squares, axis=(0, 1))
     factor = lax.rsqrt(squares / D + EPSILON)
     normed = hidden_f * factor[:, None] * norm_gain.astype(jnp.float32)[None, :]

time: 113 us -> 111 us (0.982)
  blocking collectives: 28.3 us -> 33.2 us
  waiting for transfers between devices: 15.5 us -> 11.8 us
  local copies, waits for them, and re-layouts: 2.38 us -> 0.04 us
  Pallas kernels: 16.3 us -> 14.1 us
  starting transfers between devices: 47.5 us -> 49.5 us
    ppermute x4 -> x7, starting transfers between devices: 12.3 us -> 30.4 us  [the longest x3 12.2 us: per_device(): across = lambda a, d: lax.ppermute(a, 'zl', [(i, i ^ d) for i in range(4)])]
    all_to_all x3 -> x2, starting transfers between devices: 24.4 us -> 8.94 us  [the longest x1 4.75 us: per_device(): squares = lax.all_to_all(squares, ('zl', 'c'), 0, 0, tiled=True)]
    all_to_all x3 -> x2, waiting for transfers between devices: 12 us -> 4.81 us  [the longest x1 4.81 us: per_device(): squares = lax.all_to_all(squares, ('zl', 'c'), 0, 0, tiled=True)]
    all_to_all x1, blocking collectives: 18.6 us -> 23.6 us  [per_device(): lax.all_to_all(jnp.broadcast_to(kv, (4, *kv.shape)), 'zh', 0, 0, tiled=True)]
    ppermute x4 -> x7, waiting for transfers between devices: 2.52 us -> 6.97 us  [the longest x3 4.44 us: per_device(): across = lambda a, d: lax.ppermute(a, 'zl', [(i, i ^ d) for i in range(4)])]
    broadcast_in_dim x3 -> x1, local copies, waits for them, and re-layouts: 2.36 us -> 0.02 us  [per_device(): jnp.broadcast_to(kv, (4, *kv.shape))]
    pallas_call x1, Pallas kernels: 7.75 us -> 5.54 us  [attend(): pl.pallas_call(attention_kernel, out_shape=pltpu.VMEM((peers, local + STA...]
    pallas_call x2 -> x6, Pallas kernels: 5.94 us -> 5.92 us  [the longest x2 3.14 us: columns(): pl.pallas_call(functools.partial(columns_kernel, blocks), in_specs=[pl.Bl...]
  transfers between devices with their start and end apart: 8 -> 10, of which waited for: 5 -> 5; matrix products, arithmetic and copies ran while one was open for 1% -> 1% of each run, Pallas kernels for 13% -> 12%
where the time goes in v4:
time: 111 us; the launch traced here: 110 us
  starting transfers between devices  49.5 us (45%)
  blocking collectives  33.2 us (30%)
  Pallas kernels  14.1 us (13%)
  waiting for transfers between devices  11.8 us (11%)
  other arithmetic  1.58 us (1%)
    all_to_all x1, blocking collectives, per_device(): lax.all_to_all(jnp.broadcast_to(kv, (4, *kv.shape)), 'zh', 0, 0, tiled=True)  23.6 us
    ppermute x3, starting transfers between devices, per_device(): across = lambda a, d: lax.ppermute(a, 'zl', [(i, i ^ d) for i in range(4)])  12.2 us
    ppermute x1, starting transfers between devices, per_device(): attended_other = lax.ppermute(attended, 'c', swap)  10.1 us
    all_to_all x1, blocking collectives, per_device(): parts = lax.all_to_all(parts, 'x', 0, 0, tiled=True)  9.66 us
    ppermute x3, starting transfers between devices, per_device(): lax.ppermute(a, axis, [(i, (i - d) % 4) for i in range(4)])  9.32 us
    ppermute x1, starting transfers between devices, per_device(): weight_other = lax.ppermute(out_weight, 'c', swap)  8.87 us
    pallas_call x1, Pallas kernels, attend(): pl.pallas_call(attention_kernel, out_shape=pltpu.VMEM((peers, local + STA...  5.54 us
    all_to_all x1, waiting for transfers between devices, per_device(): squares = lax.all_to_all(squares, ('zl', 'c'), 0, 0, tiled=True)  4.81 us
  transfers between devices with their start and end apart: 10, of which 5 were waited for; matrix products, arithmetic and copies ran while one was open for 1% of the time, Pallas kernels for 12%

profile of v4, /device:TPU:1, one launch (start us, length us, event | category | flops | bytes accessed | tf_op | source)
XLA Modules:
  0.0 110.4 jit_solution(13000594373311970759)
XLA Ops:
  0.0 0.0 copy-start.1
  0.0 0.0 copy-start.2
  0.0 8.9 %collective-permute-start.4 = (bf16[512,4096]{1,0:T(8,128)(2,1)}, bf16[512,4096]{1,0:T(8,128)(2,1)}, u32[]{:S(2)}, u32[]{:S(2)}) collective-permute-start(bf16[512,4096]{1,0:T(8,128)(2,1)} %w_ref.3), channel_id=1, source_target_pairs={{0,1},{1,0},{2,3},{3,2},{4,5},{5,4},{6,7},{7,6},{8,9},{9,8},{10,11... | collective-permute-start | bytes 12582920 | tf_op jit(solution)/shard_map/ppermute | solution.py:339
  8.9 0.8 pad_maximum_fusion
  9.7 23.6 %all_to_all.20 = bf16[4,128,256]{2,1,0:T(8,128)(2,1)S(1)} all-to-all(bf16[4,128,256]{2,1,0:T(8,128)(2,1)S(1)} %broadcast_in_dim.2), channel_id=1, replica_groups=mesh['y'=4,'zh'=4,'x'=4,'zl'=4,'c'=2] {'zh'}, dimensions={0} | all-to-all | bytes 524288 | tf_op jit(solution)/shard_map/all_to_all | solution.py:336
  33.3 1.0 spread.1
  34.3 4.2 %all-to-all-start.1 = ((bf16[4,512,256]{2,1,0:T(8,128)(2,1)}), bf16[4,512,256]{2,1,0:T(8,128)(2,1)S(1)}, u32[]{:S(2)}, u32[]{:S(2)}) async-start(bf16[4,512,256]{2,1,0:T(8,128)(2,1)} %spread.1), calls=%async_computation.1 | async-start | bytes 2097152 | tf_op jit(solution)/shard_map/all_to_all | solution.py:338
  38.5 0.0 copy-done.1
  38.5 4.4 %collective-permute-start = (bf16[128,512]{1,0:T(8,128)(2,1)S(1)}, bf16[128,512]{1,0:T(8,128)(2,1)S(1)}, u32[]{:S(2)}, u32[]{:S(2)}) collective-permute-start(bf16[128,512]{1,0:T(8,128)(2,1)S(1)} %copy-done.1), channel_id=1, source_target_pairs={{0,24},{8,0},{16,8},{24,16},{1,25},{9,1},{17,9},{25,17},{2,26},{10... | collective-permute-start | bytes 393224 | tf_op jit(solution)/shard_map/ppermute | solution.py:334
  42.9 2.4 %collective-permute-start.1 = (bf16[128,512]{1,0:T(8,128)(2,1)S(1)}, bf16[128,512]{1,0:T(8,128)(2,1)S(1)}, u32[]{:S(2)}, u32[]{:S(2)}) collective-permute-start(bf16[128,512]{1,0:T(8,128)(2,1)S(1)} %copy-done.1), channel_id=1, source_target_pairs={{0,16},{8,24},{16,0},{24,8},{1,17},{9,25},{17,1},{25,9},{2,18},{10... | collective-permute-start | bytes 393224 | tf_op jit(solution)/shard_map/ppermute | solution.py:334
  45.3 2.5 %collective-permute-start.2 = (bf16[128,512]{1,0:T(8,128)(2,1)S(1)}, bf16[128,512]{1,0:T(8,128)(2,1)S(1)}, u32[]{:S(2)}, u32[]{:S(2)}) collective-permute-start(bf16[128,512]{1,0:T(8,128)(2,1)S(1)} %copy-done.1), channel_id=1, source_target_pairs={{0,8},{8,16},{16,24},{24,0},{1,9},{9,17},{17,25},{25,1},{2,10},{10... | collective-permute-start | bytes 393224 | tf_op jit(solution)/shard_map/ppermute | solution.py:334
  47.8 0.0 copy-done.2
  47.8 2.1 %plan.1.tab_ref = s32[256]{0:T(256)S(1)} custom-call(s32[1]{0:T(128)} %bitcast.dev_ref, s32[128]{0:T(128)S(1)} %copy-done.2), custom_call_target="tpu_custom_call" | custom-call | tf_op jit(solution)/shard_map/plan/pallas_call | solution.py:91
  50.0 0.0 collective-permute-done.q1_ref
  50.0 0.1 collective-permute-done.1.q2_ref
  50.1 2.4 %collective-permute-done.2.q3_ref = bf16[128,512]{1,0:T(8,128)(2,1)S(1)} collective-permute-done((bf16[128,512]{1,0:T(8,128)(2,1)S(1)}, bf16[128,512]{1,0:T(8,128)(2,1)S(1)}, u32[]{:S(2)}, u32[]{:S(2)}) %collective-permute-start.2) | collective-permute-done | bytes 131104 | tf_op jit(solution)/shard_map/ppermute | solution.py:334
  52.5 0.0 all-to-all-done.1
  52.5 5.5 %attend.1 = bf16[4,144,512]{2,1,0:T(8,128)(2,1)S(1)} custom-call(s32[256]{0:T(256)S(1)} %plan.1.tab_ref, bf16[128,512]{1,0:T(8,128)(2,1)S(1)} %copy-done.1, bf16[128,512]{1,0:T(8,128)(2,1)S(1)} %collective-permute-done.q1_ref, bf16[128,512]{1,0:T(8,128)(2,1)S(1)} %collective-permute-done.1.q2_ref, bf16[128,512]{1,0:T(8,128)(2,1)S(1)} %collective-permute-done.2.q3_ref, ...), custom_call_target="tpu_custom_call" | custom-call | tf_op jit(solution)/shard_map/attend/pallas_call | solution.py:194
  58.1 9.7 %all_to_all.21.p_ref = bf16[4,144,512]{2,1,0:T(8,128)(2,1)S(1)} all-to-all(bf16[4,144,512]{2,1,0:T(8,128)(2,1)S(1)} %attend.1), channel_id=1, replica_groups=mesh['y'=4,'zh'=4,'x'=4,'zl'=4,'c'=2] {'x'}, dimensions={0} | all-to-all | bytes 1179648 | tf_op jit(solution)/shard_map/all_to_all | solution.py:342
  67.7 0.5 combine.1.own_ref
  68.3 10.1 %collective-permute-start.3 = (bf16[128,512]{1,0:T(8,128)(2,1)S(1)}, bf16[128,512]{1,0:T(8,128)(2,1)S(1)}, u32[]{:S(2)}, u32[]{:S(2)}) collective-permute-start(bf16[128,512]{1,0:T(8,128)(2,1)S(1)} %combine.1.own_ref), channel_id=1, source_target_pairs={{0,1},{1,0},{2,3},{3,2},{4,5},{5,4},{6,7},{7,6},{8,9},{9,8},{10,11... | collective-permute-start | bytes 393224 | tf_op jit(solution)/shard_map/ppermute | solution.py:346
  78.4 0.0 collective-permute-done.4.w2_ref
  78.4 1.6 %columns.3 = (bf16[512,1024]{1,0:T(8,128)(2,1)S(1)}, bf16[512,1024]{1,0:T(8,128)(2,1)S(1)}) custom-call(s32[1]{0:T(128)} %bitcast.3.at_ref, bf16[512,4096]{1,0:T(8,128)(2,1)} %w_ref.3, bf16[512,4096]{1,0:T(8,128)(2,1)} %collective-permute-done.4.w2_ref), custom_call_target="tpu_custom_call" | custom-call | tf_op jit(solution)/shard_map/columns/pallas_call | solution.py:267
  79.9 0.0 collective-permute-done.3.other_ref
  80.0 0.5 project.3
  80.4 6.8 %collective-permute-start.6 = (bf16[128,512]{1,0:T(8,128)(2,1)S(1)}, bf16[128,512]{1,0:T(8,128)(2,1)S(1)}, u32[]{:S(2)}, u32[]{:S(2)}) collective-permute-start(bf16[128,512]{1,0:T(8,128)(2,1)S(1)} %get-tuple-element.21), channel_id=1, source_target_pairs={{0,4},{2,6},{4,0},{6,2},{1,5},{3,7},{5,1},{7,3},{8,12},{10,14},{12... | collective-permute-start | bytes 393224 | tf_op jit(solution)/shard_map/ppermute | solution.py:347
  87.2 0.0 copy-start
  87.2 0.0 copy-start.3
  87.2 3.5 %collective-permute-start.7 = (bf16[128,512]{1,0:T(8,128)(2,1)S(1)}, bf16[128,512]{1,0:T(8,128)(2,1)S(1)}, u32[]{:S(2)}, u32[]{:S(2)}) collective-permute-start(bf16[128,512]{1,0:T(8,128)(2,1)S(1)} %get-tuple-element.22), channel_id=1, source_target_pairs={{0,6},{2,4},{4,2},{6,0},{1,7},{3,5},{5,3},{7,1},{8,14},{10,12},{12... | collective-permute-start | bytes 393224 | tf_op jit(solution)/shard_map/ppermute | solution.py:347
  90.8 1.6 %columns.2 = (bf16[512,1024]{1,0:T(8,128)(2,1)S(1)}, bf16[512,1024]{1,0:T(8,128)(2,1)S(1)}) custom-call(s32[1]{0:T(128)} %bitcast.3.at_ref, bf16[512,4096]{1,0:T(8,128)(2,1)} %w_ref.3, bf16[512,4096]{1,0:T(8,128)(2,1)} %collective-permute-done.4.w2_ref), custom_call_target="tpu_custom_call" | custom-call | tf_op jit(solution)/shard_map/columns/pallas_call | solution.py:267
  92.4 0.5 project.2
  92.8 1.9 %collective-permute-start.5 = (bf16[128,512]{1,0:T(8,128)(2,1)S(1)}, bf16[128,512]{1,0:T(8,128)(2,1)S(1)}, u32[]{:S(2)}, u32[]{:S(2)}) collective-permute-start(bf16[128,512]{1,0:T(8,128)(2,1)S(1)} %get-tuple-element.18), channel_id=1, source_target_pairs={{0,2},{2,0},{4,6},{6,4},{1,3},{3,1},{5,7},{7,5},{8,10},{10,8},{12,... | collective-permute-start | bytes 393224 | tf_op jit(solution)/shard_map/ppermute | solution.py:347
  94.8 0.0 collective-permute-done.6.p2_ref
  94.8 1.1 collective-permute-done.7.p3_ref
  95.9 3.3 %collective-permute-done.5.p1_ref = bf16[128,512]{1,0:T(8,128)(2,1)S(1)} collective-permute-done((bf16[128,512]{1,0:T(8,128)(2,1)S(1)}, bf16[128,512]{1,0:T(8,128)(2,1)S(1)}, u32[]{:S(2)}, u32[]{:S(2)}) %collective-permute-start.5) | collective-permute-done | bytes 131104 | tf_op jit(solution)/shard_map/ppermute | solution.py:347
  99.2 0.0 copy-done
  99.2 0.8 total.1
  100.0 4.8 %all-to-all-start.3 = ((f32[8,1,128]{2,1,0:T(1,128)}), f32[8,1,128]{2,1,0:T(1,128)S(1)}, u32[]{:S(2)}, u32[]{:S(2)}) async-start(f32[8,1,128]{2,1,0:T(1,128)} %get-tuple-element.24), calls=%async_computation.3 | async-start | bytes 8192 | tf_op jit(solution)/shard_map/all_to_all | solution.py:356
  104.8 0.0 copy-done.3
  104.8 4.8 %all-to-all-done.3 = f32[8,1,128]{2,1,0:T(1,128)S(1)} async-done(((f32[8,1,128]{2,1,0:T(1,128)}), f32[8,1,128]{2,1,0:T(1,128)S(1)}, u32[]{:S(2)}, u32[]{:S(2)}) %all-to-all-start.3) | async-done | bytes 4128 | tf_op jit(solution)/shard_map/all_to_all | solution.py:356
  109.6 0.8 multiply_convert_fusion
  (4 shorter events, 0.1 us)
Async XLA Ops:
  0.0 38.5 %copy-start.1 = (bf16[128,512]{1,0:T(8,128)(2,1)S(1)}, bf16[128,512]{1,0:T(8,128)(2,1)}, u32[]{:S(2)}) copy-start(bf16[128,512]{1,0:T(8,128)(2,1)} %q0_ref.1) | copy-start | bytes 393220
  0.0 47.8 %copy-start.2 = (s32[128]{0:T(128)S(1)}, s32[128]{0:T(128)}, u32[]{:S(2)}) copy-start(s32[128]{0:T(128)} %span_ref.1) | copy-start | bytes 1540
  0.0 78.4 %collective-permute-start.4 = (bf16[512,4096]{1,0:T(8,128)(2,1)}, bf16[512,4096]{1,0:T(8,128)(2,1)}, u32[]{:S(2)}, u32[]{:S(2)}) collective-permute-start(bf16[512,4096]{1,0:T(8,128)(2,1)} %w_ref.3), channel_id=1, source_target_pairs={{0,1},{1,0},{2,3},{3,2},{4,5},{5,4},{6,7},{7,6},{8,9},{9,8},{10,11... | collective-permute-start | bytes 12582920 | tf_op jit(solution)/shard_map/ppermute | solution.py:339
  34.3 18.2 %all-to-all-start.1 = ((bf16[4,512,256]{2,1,0:T(8,128)(2,1)}), bf16[4,512,256]{2,1,0:T(8,128)(2,1)S(1)}, u32[]{:S(2)}, u32[]{:S(2)}) async-start(bf16[4,512,256]{2,1,0:T(8,128)(2,1)} %spread.1), calls=%async_computation.1 | async-start | bytes 2097152 | tf_op jit(solution)/shard_map/all_to_all | solution.py:338
  38.5 11.5 %collective-permute-start = (bf16[128,512]{1,0:T(8,128)(2,1)S(1)}, bf16[128,512]{1,0:T(8,128)(2,1)S(1)}, u32[]{:S(2)}, u32[]{:S(2)}) collective-permute-start(bf16[128,512]{1,0:T(8,128)(2,1)S(1)} %copy-done.1), channel_id=1, source_target_pairs={{0,24},{8,0},{16,8},{24,16},{1,25},{9,1},{17,9},{25,17},{2,26},{10... | collective-permute-start | bytes 393224 | tf_op jit(solution)/shard_map/ppermute | solution.py:334
  42.9 7.2 %collective-permute-start.1 = (bf16[128,512]{1,0:T(8,128)(2,1)S(1)}, bf16[128,512]{1,0:T(8,128)(2,1)S(1)}, u32[]{:S(2)}, u32[]{:S(2)}) collective-permute-start(bf16[128,512]{1,0:T(8,128)(2,1)S(1)} %copy-done.1), channel_id=1, source_target_pairs={{0,16},{8,24},{16,0},{24,8},{1,17},{9,25},{17,1},{25,9},{2,18},{10... | collective-permute-start | bytes 393224 | tf_op jit(solution)/shard_map/ppermute | solution.py:334
  45.3 7.2 %collective-permute-start.2 = (bf16[128,512]{1,0:T(8,128)(2,1)S(1)}, bf16[128,512]{1,0:T(8,128)(2,1)S(1)}, u32[]{:S(2)}, u32[]{:S(2)}) collective-permute-start(bf16[128,512]{1,0:T(8,128)(2,1)S(1)} %copy-done.1), channel_id=1, source_target_pairs={{0,8},{8,16},{16,24},{24,0},{1,9},{9,17},{17,25},{25,1},{2,10},{10... | collective-permute-start | bytes 393224 | tf_op jit(solution)/shard_map/ppermute | solution.py:334
  68.3 11.7 %collective-permute-start.3 = (bf16[128,512]{1,0:T(8,128)(2,1)S(1)}, bf16[128,512]{1,0:T(8,128)(2,1)S(1)}, u32[]{:S(2)}, u32[]{:S(2)}) collective-permute-start(bf16[128,512]{1,0:T(8,128)(2,1)S(1)} %combine.1.own_ref), channel_id=1, source_target_pairs={{0,1},{1,0},{2,3},{3,2},{4,5},{5,4},{6,7},{7,6},{8,9},{9,8},{10,11... | collective-permute-start | bytes 393224 | tf_op jit(solution)/shard_map/ppermute | solution.py:346
  80.4 14.4 %collective-permute-start.6 = (bf16[128,512]{1,0:T(8,128)(2,1)S(1)}, bf16[128,512]{1,0:T(8,128)(2,1)S(1)}, u32[]{:S(2)}, u32[]{:S(2)}) collective-permute-start(bf16[128,512]{1,0:T(8,128)(2,1)S(1)} %get-tuple-element.21), channel_id=1, source_target_pairs={{0,4},{2,6},{4,0},{6,2},{1,5},{3,7},{5,1},{7,3},{8,12},{10,14},{12... | collective-permute-start | bytes 393224 | tf_op jit(solution)/shard_map/ppermute | solution.py:347
  87.2 12.0 %copy-start = (bf16[128,512]{1,0:T(8,128)(2,1)S(1)}, bf16[128,512]{1,0:T(8,128)(2,1)}, u32[]{:S(2)}) copy-start(bf16[128,512]{1,0:T(8,128)(2,1)} %r_ref.1) | copy-start | bytes 393220
  87.2 17.6 %copy-start.3 = (bf16[512]{0:T(512)(128)(2,1)S(1)}, bf16[512]{0:T(512)(128)(2,1)}, u32[]{:S(2)}) copy-start(bf16[512]{0:T(512)(128)(2,1)} %param.12) | copy-start | bytes 3076
  87.2 8.6 %collective-permute-start.7 = (bf16[128,512]{1,0:T(8,128)(2,1)S(1)}, bf16[128,512]{1,0:T(8,128)(2,1)S(1)}, u32[]{:S(2)}, u32[]{:S(2)}) collective-permute-start(bf16[128,512]{1,0:T(8,128)(2,1)S(1)} %get-tuple-element.22), channel_id=1, source_target_pairs={{0,6},{2,4},{4,2},{6,0},{1,7},{3,5},{5,3},{7,1},{8,14},{10,12},{12... | collective-permute-start | bytes 393224 | tf_op jit(solution)/shard_map/ppermute | solution.py:347
  92.8 6.4 %collective-permute-start.5 = (bf16[128,512]{1,0:T(8,128)(2,1)S(1)}, bf16[128,512]{1,0:T(8,128)(2,1)S(1)}, u32[]{:S(2)}, u32[]{:S(2)}) collective-permute-start(bf16[128,512]{1,0:T(8,128)(2,1)S(1)} %get-tuple-element.18), channel_id=1, source_target_pairs={{0,2},{2,0},{4,6},{6,4},{1,3},{3,1},{5,7},{7,5},{8,10},{10,8},{12,... | collective-permute-start | bytes 393224 | tf_op jit(solution)/shard_map/ppermute | solution.py:347
  100.0 9.6 %all-to-all-start.3 = ((f32[8,1,128]{2,1,0:T(1,128)}), f32[8,1,128]{2,1,0:T(1,128)S(1)}, u32[]{:S(2)}, u32[]{:S(2)}) async-start(f32[8,1,128]{2,1,0:T(1,128)} %get-tuple-element.24), calls=%async_computation.3 | async-start | bytes 8192 | tf_op jit(solution)/shard_map/all_to_all | solution.py:356
